TPU v7x, 128 devices: a whole 4x4x4 slice. The times are simulated.
128 devices in a mesh: seg: 32 (over y, x, core), col: 4 (over z).
Axes of the slice: x: 4, y: 4, z: 4, core: 2. Of those that a mesh axis runs over, the one named last changes fastest.
Arguments:
- diagonal: float32 [128, 512, 512], P('seg', None, 'col'), as said below
- lower: float32 [128, 512, 512], P('seg'), as said below
- right_side: float32 [128, 512, 512], P('seg', None, 'col'), may hold values from -0.375 to 0.375
Outputs:
- solution: float32 [128, 512, 512], P('seg', None, 'col')
Inputs may be any that keep to these rules, and one draw needn't show every extreme that they name: Every diagonal block is symmetric, and with lower it makes A symmetric positive definite. `lower`: with diagonal it makes A symmetric positive definite.
All inputs are finite; a program needn't handle non-finite values.
Results may differ from a plain program's by a relative error of at most 0.0003.
Values sent between devices are 32-bit elements; how exact they have to be, the bound alone decides.
A program may use at most 192 MiB of HBM per device.

v0:
```python
import jax
import jax.numpy as jnp
from jax import lax
from jax.sharding import PartitionSpec as P


def passed_along(shard, axis, by):
    size = lax.axis_size(axis)
    pairs = [(i, i + by) for i in range(size) if 0 <= i + by < size]
    return lax.ppermute(shard, axis, pairs)


def matmul(left_hand, right_hand):
    return jnp.dot(
        left_hand, right_hand, precision=lax.Precision.HIGHEST, preferred_element_type=jnp.float32
    )


def invert_spd(matrix):
    factor = jnp.linalg.cholesky(matrix)
    identity = jnp.eye(matrix.shape[0], dtype=jnp.float32)
    inverse_factor = lax.linalg.triangular_solve(factor, identity, left_side=True, lower=True)
    return matmul(inverse_factor.T, inverse_factor)


def backward_sweep(inverses, next_links, advanced):

    def backward(later_block, inputs):
        inverse, advanced_block, coupling = inputs
        solved = matmul(inverse, advanced_block - matmul(coupling.T, later_block))
        return (solved, solved)

    last_state, solved = lax.scan(
        backward, jnp.zeros_like(advanced[0]), (inverses, advanced, next_links), reverse=True
    )
    return solved


def on_device(diagonal, lower, right_side):
    blocks = lower.shape[0]
    block_size = lower.shape[1]
    col_share = diagonal.shape[2]
    rhs_cols = right_side.shape[2]
    interior = blocks - 1
    offset = lax.axis_index("col") * col_share
    has_left = (lax.axis_index("seg") > 0).astype(jnp.float32)
    left_block = lower[0] * has_left
    sep_block = lower[blocks - 1]
    identity = jnp.eye(block_size, dtype=jnp.float32)
    left_mask = (jnp.arange(interior) > 0).astype(jnp.float32)[:, None, None]
    couple = lower[:interior] * left_mask
    next_links = jnp.concatenate(
        [couple[1:], jnp.zeros((1, block_size, block_size), jnp.float32)], axis=0
    )
    left_cols = lax.dynamic_slice_in_dim(left_block, offset, col_share, 1)
    right_cols = lax.dynamic_slice_in_dim(sep_block, offset, col_share, 0).T
    empty_cols = jnp.zeros((interior, block_size, col_share), jnp.float32)
    stacked = jnp.concatenate(
        [
            empty_cols.at[0].set(left_cols),
            empty_cols.at[interior - 1].set(right_cols),
            right_side[:interior],
        ],
        axis=2,
    )
    diag_items = diagonal[:interior]

    def forward(state, inputs):
        inverse, previous = state
        diag_block, coupling, rhs_block = inputs
        link_rows = lax.dynamic_slice_in_dim(coupling, offset, col_share, 0)
        partial_cols = diag_block - matmul(coupling, matmul(inverse, link_rows.T))
        schur = lax.all_gather(partial_cols, "col", axis=1, tiled=True)
        new_inverse = invert_spd(schur)
        advanced = rhs_block - matmul(coupling, matmul(inverse, previous))
        return ((new_inverse, advanced), (new_inverse, advanced))

    start_state = (identity, jnp.zeros((block_size, stacked.shape[2]), jnp.float32))
    final_state, (inverses, advanced) = lax.scan(
        forward, start_state, (diag_items, couple, stacked)
    )
    solved = backward_sweep(inverses, next_links, advanced)
    own_terms = matmul(sep_block, solved[interior - 1])
    next_terms = passed_along(matmul(left_block.T, solved[0]), "seg", -1)
    pivot_block = (
        diagonal[blocks - 1] - own_terms[:, col_share : 2 * col_share] - next_terms[:, :col_share]
    )
    sub_block = -own_terms[:, :col_share]
    super_block = -next_terms[:, col_share : 2 * col_share]
    reduced_rhs = (
        right_side[blocks - 1] - own_terms[:, 2 * col_share :] - next_terms[:, 2 * col_share :]
    )
    levels = (lax.axis_size("seg") - 1).bit_length()
    for level_bit in range(levels):
        stride = 1 << level_bit
        pivot_full, sub_full, super_full = (
            lax.all_gather(pivot_block, "col", axis=1, tiled=True),
            lax.all_gather(sub_block, "col", axis=1, tiled=True),
            lax.all_gather(super_block, "col", axis=1, tiled=True),
        )
        pivot_inverse = invert_spd(pivot_full)
        scaled = matmul(
            pivot_inverse, jnp.concatenate([sub_block, super_block, reduced_rhs], axis=1)
        )
        lower_terms = passed_along(scaled, "seg", stride)
        upper_terms = passed_along(scaled, "seg", -stride)
        narrow = sub_block.shape[1]
        new_sub = -matmul(sub_full, lower_terms[:, :narrow])
        new_super = -matmul(super_full, upper_terms[:, narrow : 2 * narrow])
        pivot_block = (
            pivot_block
            - matmul(sub_full, lower_terms[:, narrow : 2 * narrow])
            - matmul(super_full, upper_terms[:, :narrow])
        )
        reduced_rhs = (
            reduced_rhs
            - matmul(sub_full, lower_terms[:, 2 * narrow :])
            - matmul(super_full, upper_terms[:, 2 * narrow :])
        )
        sub_block, super_block = (new_sub, new_super)
    pivot_full = lax.all_gather(pivot_block, "col", axis=1, tiled=True)
    separator = matmul(invert_spd(pivot_full), reduced_rhs)
    left_sep = passed_along(separator, "seg", 1)
    correction = jnp.zeros((interior, block_size, rhs_cols), jnp.float32)
    correction = correction.at[0].add(matmul(left_block, left_sep))
    correction = correction.at[interior - 1].add(matmul(sep_block.T, separator))
    previous_inverses = jnp.concatenate([identity[None], inverses[:-1]], axis=0)

    def forward_only(previous, inputs):
        inverse, coupling, rhs_block = inputs
        advanced_block = rhs_block - matmul(coupling, matmul(inverse, previous))
        return (advanced_block, advanced_block)

    last_pushed, pushed = lax.scan(
        forward_only,
        jnp.zeros((block_size, rhs_cols), jnp.float32),
        (previous_inverses, couple, correction),
    )
    adjust = backward_sweep(inverses, next_links, pushed)
    interior_part = solved[:, :, 2 * col_share :] - adjust
    return jnp.concatenate([interior_part, separator[None]], axis=0)


def solution(mesh):
    in_specs = (P("seg", None, "col"), P("seg", None, None), P("seg", None, "col"))
    out_specs = P("seg", None, "col")
    return jax.shard_map(
        on_device, mesh=mesh, in_specs=in_specs, out_specs=out_specs, check_vma=False
    )
```

profile of v0, /device:TPU:1, one launch (start us, length us, event | category | flops | bytes accessed | tf_op | source)
XLA Modules:
  0.0 1960.0 jit_solution(13351174461865648933)
XLA Ops:
  22.1 541.8 %while.87 = (s32[]{:T(128)}, f32[512,512]{1,0:T(8,128)}, f32[512,384]{1,0:T(8,128)}, f32[3,512,512]{2,1,0:T(8,128)}, f32[3,512,384]{2,1,0:T(8,128)}, /*index=5*/...) while((s32[]{:T(128)}, f32[512,512]{1,0:T(8,128)}, ...), condition=%wide.region_9.12_spmd.clone, body=%wide.region_0.11_spmd.clone.sunk | while | flops 6245581312 | bytes 71310384 | solution.py:79
  38.0 17.3 all-gather.50.cloned.1.call-done
  153.2 40.2 %custom-call.88 = f32[4,128,128]{1,2,0:T(8,128)S(1)} custom-call(f32[4,128,128]{2,1,0:T(8,128)} %get-tuple-element.1192), custom_call_target="InvertDiagBlocksLowerTriangular" | custom-call | tf_op jit(solution)/shard_map/while/body/eval_jaxpr/triangular_solve/custom-call.3 | solution.py:22
  217.3 16.1 all-gather.50.cloned.1.call-done
  331.2 40.2 %custom-call.88 = f32[4,128,128]{1,2,0:T(8,128)S(1)} custom-call(f32[4,128,128]{2,1,0:T(8,128)} %get-tuple-element.1192), custom_call_target="InvertDiagBlocksLowerTriangular" | custom-call | tf_op jit(solution)/shard_map/while/body/eval_jaxpr/triangular_solve/custom-call.3 | solution.py:22
  395.5 16.1 all-gather.50.cloned.1.call-done
  509.5 40.2 %custom-call.88 = f32[4,128,128]{1,2,0:T(8,128)S(1)} custom-call(f32[4,128,128]{2,1,0:T(8,128)} %get-tuple-element.1192), custom_call_target="InvertDiagBlocksLowerTriangular" | custom-call | tf_op jit(solution)/shard_map/while/body/eval_jaxpr/triangular_solve/custom-call.3 | solution.py:22
  566.4 23.2 %while.84 = (s32[]{:T(128)}, f32[512,384]{1,0:T(8,128)}, f32[3,512,384]{2,1,0:T(8,128)}, f32[3,512,512]{2,1,0:T(8,128)}, f32[3,512,384]{2,1,0:T(8,128)}, /*index=5*/f32[3,512,512]{2,1,0:T(8,128)}, s32[]{:T(128)}, s32[]{:T(128)}) while((s32[]{:T(128)}, f32[512,384]{1,0:T(8,128)}, f32[3,512,384]{2,1,0:T(8,128)}, f32[3,512,512]{2,1,0:T(8,128)}, ...), condition=%wide.region_11.14_spmd, body=%wide.region_10.13_spmd.sunk | while | flops 2416115712 | bytes 6817889 | solution.py:33
  613.2 20.5 %all-gather.20.cloned.1.call-done = f32[512,512]{0,1:T(8,128)} async-done(((f32[512,128]{0,1:T(8,128)}), f32[512,512]{0,1:T(8,128)}) %all-gather.20.cloned.1.call-update) | async-done | bytes 1048592 | tf_op jit(solution)/shard_map/all_gather | solution.py:97
  734.1 12.0 while.89
  746.7 40.1 %custom-call.56 = f32[4,128,128]{1,2,0:T(8,128)S(1)} custom-call(f32[4,128,128]{2,1,0:T(8,128)} %copy-done.46), custom_call_target="InvertDiagBlocksLowerTriangular" | custom-call | tf_op jit(solution)/shard_map/triangular_solve/custom-call.3 | solution.py:22
  875.1 12.1 cholesky.889
  956.6 40.1 %custom-call.60 = f32[4,128,128]{1,2,0:T(8,128)S(1)} custom-call(f32[4,128,128]{2,1,0:T(8,128)} %copy-done.47), custom_call_target="InvertDiagBlocksLowerTriangular" | custom-call | tf_op jit(solution)/shard_map/triangular_solve/custom-call.3 | solution.py:22
  1016.8 12.3 collective-permute-done.4
  1045.0 17.0 all-gather.32.cloned.1.call-done
  1144.5 12.1 cholesky.999
  1175.2 40.1 %custom-call.64 = f32[4,128,128]{1,2,0:T(8,128)S(1)} custom-call(f32[4,128,128]{2,1,0:T(8,128)} %copy-done.48), custom_call_target="InvertDiagBlocksLowerTriangular" | custom-call | tf_op jit(solution)/shard_map/triangular_solve/custom-call.3 | solution.py:22
  1236.8 12.4 collective-permute-done.6
  1264.9 30.0 %all-gather.38.cloned.1.call-done = f32[512,512]{0,1:T(8,128)} async-done(((f32[512,128]{0,1:T(8,128)}), f32[512,512]{0,1:T(8,128)}) %all-gather.38.cloned.1.call-update) | async-done | bytes 1048592 | tf_op jit(solution)/shard_map/all_gather | solution.py:97
  1326.1 12.1 cholesky.1033
  1407.7 40.1 %custom-call.68 = f32[4,128,128]{1,2,0:T(8,128)S(1)} custom-call(f32[4,128,128]{2,1,0:T(8,128)} %copy-done.49), custom_call_target="InvertDiagBlocksLowerTriangular" | custom-call | tf_op jit(solution)/shard_map/triangular_solve/custom-call.3 | solution.py:22
  1467.8 12.3 collective-permute-done.8
  1496.1 16.0 all-gather.44.cloned.1.call-done
  1594.5 11.9 cholesky.1143
  1624.9 40.1 %custom-call.72 = f32[4,128,128]{1,2,0:T(8,128)S(1)} custom-call(f32[4,128,128]{2,1,0:T(8,128)} %copy-done.50), custom_call_target="InvertDiagBlocksLowerTriangular" | custom-call | tf_op jit(solution)/shard_map/triangular_solve/custom-call.3 | solution.py:22
  1711.8 19.5 all-gather.48.cloned.1.call-done
  1790.8 13.2 cholesky.1198
  1820.6 11.9 cholesky.1215
  1839.4 13.8 while.94
  1853.2 40.8 %custom-call.76 = f32[4,128,128]{1,2,0:T(8,128)} custom-call(f32[4,128,128]{2,1,0:T(8,128)} %get-tuple-element.591), custom_call_target="InvertDiagBlocksLowerTriangular" | custom-call | tf_op jit(solution)/shard_map/triangular_solve/custom-call.3 | solution.py:22
  1919.4 14.6 while.88
  1934.1 16.0 while.85
  (746 shorter events, 1365.2 us)
Async XLA Ops:
  22.3 33.0 %all-gather.50.cloned.1.call-start = ((), (), s32[]{:S(2)}) async-start(), calls=%async_computation.16 | async-start | bytes 1310720 | tf_op jit(solution)/shard_map/while/body/eval_jaxpr/all_gather | solution.py:73
  80.0 113.4 %copy-start.2 = (f32[512,512]{1,0:T(8,128)S(1)}, f32[512,512]{1,0:T(8,128)}, u32[]{:S(2)}) copy-start(f32[512,512]{1,0:T(8,128)} %fusion.626) | copy-start | bytes 3145732 | tf_op jit(solution)/shard_map/while
  201.3 32.0 %all-gather.50.cloned.1.call-start = ((), (), s32[]{:S(2)}) async-start(), calls=%async_computation.16 | async-start | bytes 1310720 | tf_op jit(solution)/shard_map/while/body/eval_jaxpr/all_gather | solution.py:73
  379.6 32.1 %all-gather.50.cloned.1.call-start = ((), (), s32[]{:S(2)}) async-start(), calls=%async_computation.16 | async-start | bytes 1310720 | tf_op jit(solution)/shard_map/while/body/eval_jaxpr/all_gather | solution.py:73
  563.9 69.9 %all-gather.20.cloned.1.call-start = ((), (), s32[]{:S(2)}) async-start(), calls=%async_computation.1 | async-start | bytes 1310720 | tf_op jit(solution)/shard_map/all_gather | solution.py:97
  593.5 15.7 collective-permute-start
  611.6 196.7 %all-gather.22.cloned.1.call-start = ((), (), s32[]{:S(2)}) async-start(), calls=%async_computation.2 | async-start | bytes 1310720 | tf_op jit(solution)/shard_map/all_gather | solution.py:99
  612.2 206.2 %all-gather.18.cloned.1.call-start = ((), (), s32[]{:S(2)}) async-start(), calls=%async_computation | async-start | bytes 1310720 | tf_op jit(solution)/shard_map/all_gather | solution.py:98
  612.8 231.1 %all-gather.26.cloned.1.call-start = ((), (), s32[]{:S(2)}) async-start(), calls=%async_computation.4 | async-start | bytes 1310720 | tf_op jit(solution)/shard_map/all_gather | solution.py:97
  800.6 15.7 collective-permute-start.2
  805.3 13.1 collective-permute-start.1
  821.3 195.5 %all-gather.28.cloned.1.call-start = ((), (), s32[]{:S(2)}) async-start(), calls=%async_computation.5 | async-start | bytes 1310720 | tf_op jit(solution)/shard_map/all_gather | solution.py:99
  824.2 207.0 %all-gather.24.cloned.1.call-start = ((), (), s32[]{:S(2)}) async-start(), calls=%async_computation.3 | async-start | bytes 1310720 | tf_op jit(solution)/shard_map/all_gather | solution.py:98
  827.0 235.0 %all-gather.32.cloned.1.call-start = ((), (), s32[]{:S(2)}) async-start(), calls=%async_computation.7 | async-start | bytes 1310720 | tf_op jit(solution)/shard_map/all_gather | solution.py:97
  1010.6 18.5 collective-permute-start.4
  1011.9 19.3 collective-permute-start.3
  1034.1 202.7 %all-gather.34.cloned.1.call-start = ((), (), s32[]{:S(2)}) async-start(), calls=%async_computation.8 | async-start | bytes 1310720 | tf_op jit(solution)/shard_map/all_gather | solution.py:99
  1036.9 214.3 %all-gather.30.cloned.1.call-start = ((), (), s32[]{:S(2)}) async-start(), calls=%async_computation.6 | async-start | bytes 1310720 | tf_op jit(solution)/shard_map/all_gather | solution.py:98
  1039.8 255.1 %all-gather.38.cloned.1.call-start = ((), (), s32[]{:S(2)}) async-start(), calls=%async_computation.10 | async-start | bytes 1310720 | tf_op jit(solution)/shard_map/all_gather | solution.py:97
  1229.1 20.0 %collective-permute-start.6 = (f32[512,384]{1,0:T(8,128)}, f32[512,384]{1,0:T(8,128)}, u32[]{:S(2)}, u32[]{:S(2)}) collective-permute-start(f32[512,384]{1,0:T(8,128)} %fusion.181), channel_id=1, source_target_pairs={{16,0},{20,4},{24,8},{28,12},{32,16},{36,20},{40,24},{44,28},{48,3... | collective-permute-start | bytes 2359304 | tf_op jit(solution)/shard_map/ppermute | solution.py:10
  1230.4 20.9 %collective-permute-start.5 = (f32[512,384]{1,0:T(8,128)}, f32[512,384]{1,0:T(8,128)}, u32[]{:S(2)}, u32[]{:S(2)}) collective-permute-start(f32[512,384]{1,0:T(8,128)} %fusion.181), channel_id=1, source_target_pairs={{0,16},{4,20},{8,24},{12,28},{16,32},{20,36},{24,40},{28,44},{32,4... | collective-permute-start | bytes 2359304 | tf_op jit(solution)/shard_map/ppermute | solution.py:10
  1254.2 213.6 %all-gather.40.cloned.1.call-start = ((), (), s32[]{:S(2)}) async-start(), calls=%async_computation.11 | async-start | bytes 1310720 | tf_op jit(solution)/shard_map/all_gather | solution.py:99
  1257.0 225.2 %all-gather.36.cloned.1.call-start = ((), (), s32[]{:S(2)}) async-start(), calls=%async_computation.9 | async-start | bytes 1310720 | tf_op jit(solution)/shard_map/all_gather | solution.py:98
  1259.8 252.2 %all-gather.44.cloned.1.call-start = ((), (), s32[]{:S(2)}) async-start(), calls=%async_computation.13 | async-start | bytes 1310720 | tf_op jit(solution)/shard_map/all_gather | solution.py:97
  1461.6 18.5 collective-permute-start.8
  1462.9 19.3 collective-permute-start.7
  1485.1 202.7 %all-gather.46.cloned.1.call-start = ((), (), s32[]{:S(2)}) async-start(), calls=%async_computation.14 | async-start | bytes 1310720 | tf_op jit(solution)/shard_map/all_gather | solution.py:99
  1488.0 213.0 %all-gather.42.cloned.1.call-start = ((), (), s32[]{:S(2)}) async-start(), calls=%async_computation.12 | async-start | bytes 1310720 | tf_op jit(solution)/shard_map/all_gather | solution.py:98
  1490.8 240.6 %all-gather.48.cloned.1.call-start = ((), (), s32[]{:S(2)}) async-start(), calls=%async_computation.15 | async-start | bytes 1310720 | tf_op jit(solution)/shard_map/all_gather | solution.py:121
  1678.8 20.0 %collective-permute-start.10 = (f32[512,384]{1,0:T(8,128)}, f32[512,384]{1,0:T(8,128)}, u32[]{:S(2)}, u32[]{:S(2)}) collective-permute-start(f32[512,384]{1,0:T(8,128)} %fusion.203), channel_id=1, source_target_pairs={{64,0},{68,4},{72,8},{76,12},{80,16},{84,20},{88,24},{92,28},{96,3... | collective-permute-start | bytes 2359304 | tf_op jit(solution)/shard_map/ppermute | solution.py:10
  1680.1 20.8 %collective-permute-start.9 = (f32[512,384]{1,0:T(8,128)}, f32[512,384]{1,0:T(8,128)}, u32[]{:S(2)}, u32[]{:S(2)}) collective-permute-start(f32[512,384]{1,0:T(8,128)} %fusion.203), channel_id=1, source_target_pairs={{0,64},{4,68},{8,72},{12,76},{16,80},{20,84},{24,88},{28,92},{32,9... | collective-permute-start | bytes 2359304 | tf_op jit(solution)/shard_map/ppermute | solution.py:10
  1905.1 9.1 collective-permute-start.11
  (60 other events, 655.5 us)
Sparse Core Ops, SparseCore 0:
  29.8 25.4 all-gather.49
  208.8 24.5 all-gather.49
  387.1 24.5 all-gather.49
Sparse Core Ops, SparseCore 1:
  611.7 22.0 all-gather.19
  635.3 24.6 all-gather.21
  661.4 24.6 all-gather.17
  821.4 22.4 all-gather.25
  845.6 24.7 all-gather.27
  872.0 24.5 all-gather.23
  1034.2 27.8 all-gather.31
  1063.5 24.6 all-gather.33
  1089.7 24.6 all-gather.29
  1254.2 40.6 all-gather.37
  1296.4 24.6 all-gather.39
  1322.8 24.6 all-gather.35
  1485.2 26.8 all-gather.43
  1513.8 24.5 all-gather.45
  1540.0 24.6 all-gather.41
  1703.9 27.4 all-gather.47
where the time goes:
time: 1970 us; the launch traced here: 1960 us
  other arithmetic  1140 us (58%)
  matrix products  331 us (17%)
  waiting for transfers between devices  226 us (11%)
  local copies, waits for them, and re-layouts  169 us (9%)
  starting transfers between devices  49.7 us (3%)
  between operations  32.2 us (2%)
    another operation x131, other arithmetic, invert_spd(): factor = jnp.linalg.cholesky(matrix)  727 us
    another operation x25, other arithmetic, invert_spd(): lax.linalg.triangular_solve(factor, identity, left_side=True, lower=True)  377 us
    dot_general x77, matrix products, matmul(): jnp.dot(left_hand, right_hand, precision=lax.Precision.HIGHEST, preferred...  210 us
    another operation x118, local copies, waits for them, and re-layouts, invert_spd(): lax.linalg.triangular_solve(factor, identity, left_side=True, lower=True)  105 us
    all_gather x5, waiting for transfers between devices, on_device(): lax.all_gather(pivot_block, 'col', axis=1, tiled=True)  95.3 us
    another operation x63, matrix products, invert_spd(): lax.linalg.triangular_solve(factor, identity, left_side=True, lower=True)  66 us
    ppermute x12, waiting for transfers between devices, passed_along(): return lax.ppermute(shard, axis, pairs)  59.6 us
    another operation x54, matrix products, invert_spd(): factor = jnp.linalg.cholesky(matrix)  55.1 us
  transfers between devices with their start and end apart: 31, of which 16 were waited for; matrix products, arithmetic and copies ran while one was open for 46% of the time, Pallas kernels for 0%

commit v1 on v0

--- a/solution.py
+++ b/solution.py
@@ -1,6 +1,8 @@
 import jax
 import jax.numpy as jnp
 from jax import lax
+from jax.experimental import pallas as pl
+from jax.experimental.pallas import tpu as pltpu
 from jax.sharding import PartitionSpec as P
 
 
@@ -16,11 +18,71 @@
     )
 
 
+W = 16
+
+def invert_panel(lanes, block, k):
+    first = W * k
+    tiles = W // 8
+    rows = jnp.concatenate(block[tiles * k: tiles * (k + 1)], axis=0)
+    cols = [jnp.broadcast_to(rows[:, first + p: first + p + 1], (W, 128)) for p in range(W)]
+    others = [i for i in range(16) if not tiles * k <= i < tiles * (k + 1)]
+    wide = {i: [jnp.broadcast_to(block[i][:, first + p: first + p + 1], (8, 128)) for p in range(W)] for i in others}
+    inside = (lanes >= first) & (lanes < first + W)
+    sub16 = lax.broadcasted_iota(jnp.int32, (W, 128), 0)
+    lane16 = lax.broadcasted_iota(jnp.int32, (W, 128), 1)
+    rows = jnp.where((lane16 >= first) & (lane16 < first + W), (lane16 - first == sub16).astype(jnp.float32), rows)
+    for p in range(W):
+        pivot = 1.0 / cols[p][p:p + 1, :]
+        here = sub16 == p
+        scaled = rows[p:p + 1, :] * pivot
+        rows = jnp.where(here, scaled, rows - cols[p] * scaled)
+        for j in range(p + 1, W):
+            scaled_j = cols[j][p:p + 1, :] * pivot
+            cols[j] = jnp.where(here, scaled_j, cols[j] - cols[p] * scaled_j)
+    out = [None] * 16
+    for i in range(tiles):
+        out[tiles * k + i] = rows[8 * i: 8 * i + 8]
+    for i in others:
+        acc = jnp.where(inside, 0.0, block[i])
+        for p in range(W):
+            acc = acc - wide[i][p] * rows[p:p + 1, :]
+        out[i] = acc
+    return out
+
+def invert128(block):
+    lanes = lax.broadcasted_iota(jnp.int32, (8, 128), 1)
+    tiles = [block[8 * i: 8 * i + 8] for i in range(16)]
+    for k in range(128 // W):
+        tiles = invert_panel(lanes, tiles, k)
+    return jnp.concatenate(tiles, axis=0)
+
+def k512(x, o):
+    o[...] = x[...]
+    def step(j, c):
+        s = pl.ds(pl.multiple_of(j * 128, 128), 128)
+        w = invert128(o[s, s])
+        row = o[s, :]
+        t = matmul(w, row)
+        col = o[:, s]
+        rowid = lax.broadcasted_iota(jnp.int32, (512, 1), 0) // 128
+        u = jnp.where(rowid == j, 0.0, col)
+        o[:, s] = jnp.zeros((512, 128), jnp.float32)
+        lane = lax.broadcasted_iota(jnp.int32, (1, 512), 1) // 128
+        wt = jnp.concatenate([w] * 4, axis=1)
+        t = jnp.where(lane == j, wt, t)
+        o[...] = o[...] - matmul(u, t)
+        o[s, :] = t
+        return c
+    lax.fori_loop(0, 4, step, 0)
+
+
 def invert_spd(matrix):
-    factor = jnp.linalg.cholesky(matrix)
-    identity = jnp.eye(matrix.shape[0], dtype=jnp.float32)
-    inverse_factor = lax.linalg.triangular_solve(factor, identity, left_side=True, lower=True)
-    return matmul(inverse_factor.T, inverse_factor)
+    return pl.pallas_call(
+        k512,
+        out_shape=jax.ShapeDtypeStruct(matrix.shape, jnp.float32),
+        in_specs=[pl.BlockSpec(memory_space=pltpu.VMEM)],
+        out_specs=pl.BlockSpec(memory_space=pltpu.VMEM),
+    )(matrix)
 
 
 def backward_sweep(inverses, next_links, advanced):

time: 1970 us -> 797 us (0.40)
  other arithmetic: 1140 us -> 13.3 us
  Pallas kernels: 0 us -> 222 us
  local copies, waits for them, and re-layouts: 169 us -> 17.5 us
  matrix products: 331 us -> 199 us
  waiting for transfers between devices: 226 us -> 269 us
    another operation x156 -> x0, other arithmetic: 1100 us -> none  [the longest x131 727 us: invert_spd(): factor = jnp.linalg.cholesky(matrix)]
    pallas_call x0 -> x9, Pallas kernels: none -> 222 us  [invert_spd(): pl.pallas_call(k512, out_shape=jax.ShapeDtypeStruct(matrix.shape, jnp.flo...]
    another operation x117 -> x0, matrix products: 121 us -> none  [the longest x63 66 us: invert_spd(): lax.linalg.triangular_solve(factor, identity, left_side=True, lower=True)]
    another operation x160 -> x6, local copies, waits for them, and re-layouts: 118 us -> 6.05 us  [the longest x118 105 us: invert_spd(): lax.linalg.triangular_solve(factor, identity, left_side=True, lower=True)]
    all_gather x5, waiting for transfers between devices: 0.13 us -> 25.3 us  [on_device(): lax.all_gather(sub_block, 'col', axis=1, tiled=True)]
    all_gather x9 -> x0, local copies, waits for them, and re-layouts: 19.9 us -> none  [the longest x5 12.7 us: on_device(): lax.all_gather(pivot_block, 'col', axis=1, tiled=True)]
    dot_general x77 -> x68, matrix products: 210 us -> 199 us  [matmul(): jnp.dot(left_hand, right_hand, precision=lax.Precision.HIGHEST, preferred...]
  transfers between devices with their start and end apart: 31 -> 31, of which waited for: 16 -> 21; matrix products, arithmetic and copies ran while one was open for 46% -> 14% of each run, Pallas kernels for 0% -> 16%
where the time goes in v1:
time: 797 us; the launch traced here: 784 us
  waiting for transfers between devices  269 us (34%)
  Pallas kernels  222 us (28%)
  matrix products  199 us (25%)
  starting transfers between devices  46.7 us (6%)
  local copies, waits for them, and re-layouts  17.5 us (2%)
  between operations  15.6 us (2%)
  other arithmetic  13.3 us (2%)
    pallas_call x9, Pallas kernels, invert_spd(): pl.pallas_call(k512, out_shape=jax.ShapeDtypeStruct(matrix.shape, jnp.flo...  222 us
    dot_general x68, matrix products, matmul(): jnp.dot(left_hand, right_hand, precision=lax.Precision.HIGHEST, preferred...  199 us
    all_gather x5, waiting for transfers between devices, on_device(): lax.all_gather(pivot_block, 'col', axis=1, tiled=True)  94.2 us
    ppermute x12, waiting for transfers between devices, passed_along(): return lax.ppermute(shard, axis, pairs)  67.8 us
    all_gather x3, waiting for transfers between devices, forward(): schur = lax.all_gather(partial_cols, 'col', axis=1, tiled=True)  62.8 us
    ppermute x12, starting transfers between devices, passed_along(): return lax.ppermute(shard, axis, pairs)  45 us
    all_gather x5, waiting for transfers between devices, on_device(): lax.all_gather(sub_block, 'col', axis=1, tiled=True)  25.3 us
    all_gather x1, waiting for transfers between devices, on_device(): pivot_full = lax.all_gather(pivot_block, 'col', axis=1, tiled=True)  17.9 us
  transfers between devices with their start and end apart: 31, of which 21 were waited for; matrix products, arithmetic and copies ran while one was open for 14% of the time, Pallas kernels for 16%

profile of v1, /device:TPU:1, one launch (start us, length us, event | category | flops | bytes accessed | tf_op | source)
XLA Modules:
  0.0 784.0 jit_solution(479957845891825087)
XLA Ops:
  19.3 171.4 %while.71 = (s32[]{:T(128)}, f32[512,512]{1,0:T(8,128)S(1)}, f32[512,384]{1,0:T(8,128)S(1)}, f32[3,512,512]{2,1,0:T(8,128)}, f32[3,512,384]{2,1,0:T(8,128)}, /*i...) while((s32[]{:T(128)}, f32[512,512]{1,0:T(8,128)S(1)}, ...), condition=%wide.region_1.0_spmd.clone, body=%wide.region_0.0_spmd.clone.sunk | while | flops 3221684224 | bytes 16255687 | solution.py:141
  30.4 21.7 %all-gather.50.cloned.1.call-done.x = f32[512,512]{1,0:T(8,128)} async-done(((f32[512,128]{1,0:T(8,128)}), f32[512,512]{1,0:T(8,128)}) %all-gather.50.cloned.1.call-update) | async-done | bytes 1048592 | tf_op jit(solution)/shard_map/while/body/eval_jaxpr/all_gather | solution.py:135
  52.0 24.0 %eval_jaxpr.5 = f32[512,512]{1,0:T(8,128)S(1)} custom-call(f32[512,512]{1,0:T(8,128)} %all-gather.50.cloned.1.call-done.x), custom_call_target="tpu_custom_call" | custom-call | tf_op jit(solution)/shard_map/while/body/eval_jaxpr/pallas_call | solution.py:80
  88.2 20.6 %all-gather.50.cloned.1.call-done.x = f32[512,512]{1,0:T(8,128)} async-done(((f32[512,128]{1,0:T(8,128)}), f32[512,512]{1,0:T(8,128)}) %all-gather.50.cloned.1.call-update) | async-done | bytes 1048592 | tf_op jit(solution)/shard_map/while/body/eval_jaxpr/all_gather | solution.py:135
  108.8 24.0 %eval_jaxpr.5 = f32[512,512]{1,0:T(8,128)S(1)} custom-call(f32[512,512]{1,0:T(8,128)} %all-gather.50.cloned.1.call-done.x), custom_call_target="tpu_custom_call" | custom-call | tf_op jit(solution)/shard_map/while/body/eval_jaxpr/pallas_call | solution.py:80
  145.0 20.6 %all-gather.50.cloned.1.call-done.x = f32[512,512]{1,0:T(8,128)} async-done(((f32[512,128]{1,0:T(8,128)}), f32[512,512]{1,0:T(8,128)}) %all-gather.50.cloned.1.call-update) | async-done | bytes 1048592 | tf_op jit(solution)/shard_map/while/body/eval_jaxpr/all_gather | solution.py:135
  165.6 24.0 %eval_jaxpr.5 = f32[512,512]{1,0:T(8,128)S(1)} custom-call(f32[512,512]{1,0:T(8,128)} %all-gather.50.cloned.1.call-done.x), custom_call_target="tpu_custom_call" | custom-call | tf_op jit(solution)/shard_map/while/body/eval_jaxpr/pallas_call | solution.py:80
  193.7 22.4 %while.69 = (s32[]{:T(128)}, f32[512,384]{1,0:T(8,128)}, f32[3,512,384]{2,1,0:T(8,128)}, f32[3,512,512]{2,1,0:T(8,128)}, f32[3,512,384]{2,1,0:T(8,128)}, /*index=5*/f32[3,512,512]{2,1,0:T(8,128)S(1)}, s32[]{:T(128)}, s32[]{:T(128)}) while((s32[]{:T(128)}, f32[512,384]{1,0:T(8,128)}, f32[3,512,384]{2,1,0:T(8,128)}, f32[3,512,512]{2,1,0:T(8,128)}, ...), condition=%wide.region_3.4_spmd, body=%wide.region_2.3_spmd.sunk | while | flops 2416115712 | bytes 6817889 | solution.py:95
  226.6 7.4 collective-permute-done
  237.2 23.7 %all-gather.20.cloned.1.call-done.x = f32[512,512]{1,0:T(8,128)} async-done(((f32[512,128]{1,0:T(8,128)}), f32[512,512]{1,0:T(8,128)}) %all-gather.20.cloned.1.call-update) | async-done | bytes 1048592 | tf_op jit(solution)/shard_map/all_gather | solution.py:159
  260.9 25.4 %shard_map.37 = f32[512,512]{1,0:T(8,128)} custom-call(f32[512,512]{1,0:T(8,128)} %all-gather.20.cloned.1.call-done.x), custom_call_target="tpu_custom_call" | custom-call | tf_op jit(solution)/shard_map/pallas_call | solution.py:80
  297.2 8.3 %collective-permute-done.2 = f32[512,384]{1,0:T(8,128)} collective-permute-done((f32[512,384]{1,0:T(8,128)}, f32[512,384]{1,0:T(8,128)}, u32[]{:S(2)}, u32[]{:S(2)}) %collective-permute-start.2) | collective-permute-done | bytes 786464 | tf_op jit(solution)/shard_map/ppermute | solution.py:12
  308.5 7.9 %all-gather.18.cloned.1.call-done = f32[512,512]{1,0:T(8,128)} async-done(((f32[512,128]{1,0:T(8,128)}), f32[512,512]{1,0:T(8,128)}) %all-gather.18.cloned.1.call-update) | async-done | bytes 1048592 | tf_op jit(solution)/shard_map/all_gather | solution.py:160
  331.2 14.7 %all-gather.26.cloned.1.call-done.x = f32[512,512]{1,0:T(8,128)} async-done(((f32[512,128]{1,0:T(8,128)}), f32[512,512]{1,0:T(8,128)}) %all-gather.26.cloned.1.call-update) | async-done | bytes 1048592 | tf_op jit(solution)/shard_map/all_gather | solution.py:159
  345.9 25.0 %shard_map.38 = f32[512,512]{1,0:T(8,128)} custom-call(f32[512,512]{1,0:T(8,128)} %all-gather.26.cloned.1.call-done.x), custom_call_target="tpu_custom_call" | custom-call | tf_op jit(solution)/shard_map/pallas_call | solution.py:80
  381.2 13.1 %collective-permute-done.4 = f32[512,384]{1,0:T(8,128)} collective-permute-done((f32[512,384]{1,0:T(8,128)}, f32[512,384]{1,0:T(8,128)}, u32[]{:S(2)}, u32[]{:S(2)}) %collective-permute-start.4) | collective-permute-done | bytes 786464 | tf_op jit(solution)/shard_map/ppermute | solution.py:12
  416.6 14.5 %all-gather.32.cloned.1.call-done.x = f32[512,512]{1,0:T(8,128)} async-done(((f32[512,128]{1,0:T(8,128)}), f32[512,512]{1,0:T(8,128)}) %all-gather.32.cloned.1.call-update) | async-done | bytes 1048592 | tf_op jit(solution)/shard_map/all_gather | solution.py:159
  431.1 25.0 %shard_map.39 = f32[512,512]{1,0:T(8,128)} custom-call(f32[512,512]{1,0:T(8,128)} %all-gather.32.cloned.1.call-done.x), custom_call_target="tpu_custom_call" | custom-call | tf_op jit(solution)/shard_map/pallas_call | solution.py:80
  461.5 6.6 collective-permute-start.5
  468.1 12.9 %collective-permute-done.6 = f32[512,384]{1,0:T(8,128)} collective-permute-done((f32[512,384]{1,0:T(8,128)}, f32[512,384]{1,0:T(8,128)}, u32[]{:S(2)}, u32[]{:S(2)}) %collective-permute-start.6) | collective-permute-done | bytes 786464 | tf_op jit(solution)/shard_map/ppermute | solution.py:12
  501.2 26.9 %all-gather.38.cloned.1.call-done.x = f32[512,512]{1,0:T(8,128)} async-done(((f32[512,128]{1,0:T(8,128)}), f32[512,512]{1,0:T(8,128)}) %all-gather.38.cloned.1.call-update) | async-done | bytes 1048592 | tf_op jit(solution)/shard_map/all_gather | solution.py:159
  528.1 25.0 %shard_map.40 = f32[512,512]{1,0:T(8,128)} custom-call(f32[512,512]{1,0:T(8,128)} %all-gather.38.cloned.1.call-done.x), custom_call_target="tpu_custom_call" | custom-call | tf_op jit(solution)/shard_map/pallas_call | solution.py:80
  563.3 13.1 %collective-permute-done.8 = f32[512,384]{1,0:T(8,128)} collective-permute-done((f32[512,384]{1,0:T(8,128)}, f32[512,384]{1,0:T(8,128)}, u32[]{:S(2)}, u32[]{:S(2)}) %collective-permute-start.8) | collective-permute-done | bytes 786464 | tf_op jit(solution)/shard_map/ppermute | solution.py:12
  598.7 14.5 %all-gather.44.cloned.1.call-done.x = f32[512,512]{1,0:T(8,128)} async-done(((f32[512,128]{1,0:T(8,128)}), f32[512,512]{1,0:T(8,128)}) %all-gather.44.cloned.1.call-update) | async-done | bytes 1048592 | tf_op jit(solution)/shard_map/all_gather | solution.py:159
  613.2 25.0 %shard_map.41 = f32[512,512]{1,0:T(8,128)} custom-call(f32[512,512]{1,0:T(8,128)} %all-gather.44.cloned.1.call-done.x), custom_call_target="tpu_custom_call" | custom-call | tf_op jit(solution)/shard_map/pallas_call | solution.py:80
  643.6 7.4 collective-permute-start.9
  651.0 12.0 %collective-permute-done.10 = f32[512,384]{1,0:T(8,128)} collective-permute-done((f32[512,384]{1,0:T(8,128)}, f32[512,384]{1,0:T(8,128)}, u32[]{:S(2)}, u32[]{:S(2)}) %collective-permute-start.10) | collective-permute-done | bytes 786464 | tf_op jit(solution)/shard_map/ppermute | solution.py:12
  680.5 17.9 %all-gather.48.cloned.1.call-done.x = f32[512,512]{1,0:T(8,128)} async-done(((f32[512,128]{1,0:T(8,128)}), f32[512,512]{1,0:T(8,128)}) %all-gather.48.cloned.1.call-update) | async-done | bytes 1048592 | tf_op jit(solution)/shard_map/all_gather | solution.py:183
  698.4 25.0 %shard_map.42 = f32[512,512]{1,0:T(8,128)} custom-call(f32[512,512]{1,0:T(8,128)} %all-gather.48.cloned.1.call-done.x), custom_call_target="tpu_custom_call" | custom-call | tf_op jit(solution)/shard_map/pallas_call | solution.py:80
  725.8 5.2 collective-permute-start.11
  739.4 15.6 %while.72 = (s32[]{:T(128)}, f32[512,128]{1,0:T(8,128)S(1)}, f32[3,512,128]{2,1,0:T(8,128)}, f32[3,512,128]{2,1,0:T(8,128)}, f32[3,512,512]{2,1,0:T(8,128)}, /*index=5*/f32[3,512,512]{2,1,0:T(8,128)}, s32[]{:T(128)}, s32[]{:T(128)}) while((s32[]{:T(128)}, f32[512,128]{1,0:T(8,128)S(1)}, f32[3,512,128]{2,1,0:T(8,128)}, ...), condition=%wide.region_5.6_spmd.clone, body=%wide.region_4.5_spmd.clone.sunk | while | flops 805437440 | bytes 3671647 | solution.py:196
  755.9 17.1 %while.70 = (s32[]{:T(128)}, f32[512,128]{1,0:T(8,128)S(1)}, f32[3,512,128]{2,1,0:T(8,128)}, f32[3,512,512]{2,1,0:T(8,128)}, f32[3,512,128]{2,1,0:T(8,128)}, /*i...) while((s32[]{:T(128)}, f32[512,128]{1,0:T(8,128)S(1)}, f32[3,512,128]{2,1,0:T(8,128)}, ...), condition=%wide.region_7.8_spmd, body=%wide.region_6.7_spmd.sunk | while | flops 805371904 | bytes 3672161 | solution.py:95
  (190 shorter events, 276.8 us)
Async XLA Ops:
  19.3 32.8 %all-gather.50.cloned.1.call-start = ((), (), s32[]{:S(2)}) async-start(), calls=%async_computation.16 | async-start | bytes 1310720 | tf_op jit(solution)/shard_map/while/body/eval_jaxpr/all_gather | solution.py:135
  77.2 31.6 %all-gather.50.cloned.1.call-start = ((), (), s32[]{:S(2)}) async-start(), calls=%async_computation.16 | async-start | bytes 1310720 | tf_op jit(solution)/shard_map/while/body/eval_jaxpr/all_gather | solution.py:135
  133.9 31.6 %all-gather.50.cloned.1.call-start = ((), (), s32[]{:S(2)}) async-start(), calls=%async_computation.16 | async-start | bytes 1310720 | tf_op jit(solution)/shard_map/while/body/eval_jaxpr/all_gather | solution.py:135
  190.7 70.2 %all-gather.20.cloned.1.call-start = ((), (), s32[]{:S(2)}) async-start(), calls=%async_computation.1 | async-start | bytes 1310720 | tf_op jit(solution)/shard_map/all_gather | solution.py:159
  219.4 14.6 %collective-permute-start = (f32[512,384]{1,0:T(8,128)S(1)}, f32[512,384]{1,0:T(8,128)S(1)}, u32[]{:S(2)}, u32[]{:S(2)}) collective-permute-start(f32[512,384]{1,0:T(8,128)S(1)} %fusion.56), channel_id=1, source_target_pairs={{4,0},{8,4},{12,8},{16,12},{20,16},{24,20},{28,24},{32,28},{36,32}... | collective-permute-start | bytes 2359304 | tf_op jit(solution)/shard_map/ppermute | solution.py:12
  235.9 72.6 %copy-start.11 = (f32[512,128]{1,0:T(8,128)}, f32[512,128]{1,0:T(8,128)S(1)}, u32[]{:S(2)}) copy-start(f32[512,128]{1,0:T(8,128)S(1)} %get-tuple-element.603) | copy-start | bytes 786436
  236.0 61.3 %all-gather.22.cloned.1.call-start = ((), (), s32[]{:S(2)}) async-start(), calls=%async_computation.2 | async-start | bytes 1310720 | tf_op jit(solution)/shard_map/all_gather | solution.py:161
  236.6 79.8 %all-gather.18.cloned.1.call-start = ((), (), s32[]{:S(2)}) async-start(), calls=%async_computation | async-start | bytes 1310720 | tf_op jit(solution)/shard_map/all_gather | solution.py:160
  237.1 108.7 %all-gather.26.cloned.1.call-start = ((), (), s32[]{:S(2)}) async-start(), calls=%async_computation.4 | async-start | bytes 1310720 | tf_op jit(solution)/shard_map/all_gather | solution.py:159
  290.3 15.3 %collective-permute-start.2 = (f32[512,384]{1,0:T(8,128)}, f32[512,384]{1,0:T(8,128)}, u32[]{:S(2)}, u32[]{:S(2)}) collective-permute-start(f32[512,384]{1,0:T(8,128)} %fusion.60), channel_id=1, source_target_pairs={{4,0},{8,4},{12,8},{16,12},{20,16},{24,20},{28,24},{32,28},{36,32}... | collective-permute-start | bytes 2359304 | tf_op jit(solution)/shard_map/ppermute | solution.py:12
  294.2 22.2 %collective-permute-start.1 = (f32[512,384]{1,0:T(8,128)}, f32[512,384]{1,0:T(8,128)}, u32[]{:S(2)}, u32[]{:S(2)}) collective-permute-start(f32[512,384]{1,0:T(8,128)} %fusion.60), channel_id=1, source_target_pairs={{0,4},{4,8},{8,12},{12,16},{16,20},{20,24},{24,28},{28,32},{32,36}... | collective-permute-start | bytes 2359304 | tf_op jit(solution)/shard_map/ppermute | solution.py:12
  319.6 61.6 %all-gather.28.cloned.1.call-start = ((), (), s32[]{:S(2)}) async-start(), calls=%async_computation.5 | async-start | bytes 1310720 | tf_op jit(solution)/shard_map/all_gather | solution.py:161
  322.6 79.1 %all-gather.24.cloned.1.call-start = ((), (), s32[]{:S(2)}) async-start(), calls=%async_computation.3 | async-start | bytes 1310720 | tf_op jit(solution)/shard_map/all_gather | solution.py:160
  325.6 105.5 %all-gather.32.cloned.1.call-start = ((), (), s32[]{:S(2)}) async-start(), calls=%async_computation.7 | async-start | bytes 1310720 | tf_op jit(solution)/shard_map/all_gather | solution.py:159
  375.0 19.3 %collective-permute-start.4 = (f32[512,384]{1,0:T(8,128)}, f32[512,384]{1,0:T(8,128)}, u32[]{:S(2)}, u32[]{:S(2)}) collective-permute-start(f32[512,384]{1,0:T(8,128)} %fusion.66), channel_id=1, source_target_pairs={{8,0},{12,4},{16,8},{20,12},{24,16},{28,20},{32,24},{36,28},{40,32... | collective-permute-start | bytes 2359304 | tf_op jit(solution)/shard_map/ppermute | solution.py:12
  376.2 25.5 %collective-permute-start.3 = (f32[512,384]{1,0:T(8,128)}, f32[512,384]{1,0:T(8,128)}, u32[]{:S(2)}, u32[]{:S(2)}) collective-permute-start(f32[512,384]{1,0:T(8,128)} %fusion.66), channel_id=1, source_target_pairs={{0,8},{4,12},{8,16},{12,20},{16,24},{20,28},{24,32},{28,36},{32,40... | collective-permute-start | bytes 2359304 | tf_op jit(solution)/shard_map/ppermute | solution.py:12
  404.8 63.3 %all-gather.34.cloned.1.call-start = ((), (), s32[]{:S(2)}) async-start(), calls=%async_computation.8 | async-start | bytes 1310720 | tf_op jit(solution)/shard_map/all_gather | solution.py:161
  408.2 78.4 %all-gather.30.cloned.1.call-start = ((), (), s32[]{:S(2)}) async-start(), calls=%async_computation.6 | async-start | bytes 1310720 | tf_op jit(solution)/shard_map/all_gather | solution.py:160
  411.3 116.8 %all-gather.38.cloned.1.call-start = ((), (), s32[]{:S(2)}) async-start(), calls=%async_computation.10 | async-start | bytes 1310720 | tf_op jit(solution)/shard_map/all_gather | solution.py:159
  460.2 20.8 %collective-permute-start.6 = (f32[512,384]{1,0:T(8,128)}, f32[512,384]{1,0:T(8,128)}, u32[]{:S(2)}, u32[]{:S(2)}) collective-permute-start(f32[512,384]{1,0:T(8,128)} %fusion.72), channel_id=1, source_target_pairs={{16,0},{20,4},{24,8},{28,12},{32,16},{36,20},{40,24},{44,28},{48,3... | collective-permute-start | bytes 2359304 | tf_op jit(solution)/shard_map/ppermute | solution.py:12
  461.5 25.2 %collective-permute-start.5 = (f32[512,384]{1,0:T(8,128)}, f32[512,384]{1,0:T(8,128)}, u32[]{:S(2)}, u32[]{:S(2)}) collective-permute-start(f32[512,384]{1,0:T(8,128)} %fusion.72), channel_id=1, source_target_pairs={{0,16},{4,20},{8,24},{12,28},{16,32},{20,36},{24,40},{28,44},{32,4... | collective-permute-start | bytes 2359304 | tf_op jit(solution)/shard_map/ppermute | solution.py:12
  489.7 73.6 %all-gather.40.cloned.1.call-start = ((), (), s32[]{:S(2)}) async-start(), calls=%async_computation.11 | async-start | bytes 1310720 | tf_op jit(solution)/shard_map/all_gather | solution.py:161
  492.8 91.0 %all-gather.36.cloned.1.call-start = ((), (), s32[]{:S(2)}) async-start(), calls=%async_computation.9 | async-start | bytes 1310720 | tf_op jit(solution)/shard_map/all_gather | solution.py:160
  495.8 117.4 %all-gather.44.cloned.1.call-start = ((), (), s32[]{:S(2)}) async-start(), calls=%async_computation.13 | async-start | bytes 1310720 | tf_op jit(solution)/shard_map/all_gather | solution.py:159
  557.1 19.3 %collective-permute-start.8 = (f32[512,384]{1,0:T(8,128)}, f32[512,384]{1,0:T(8,128)}, u32[]{:S(2)}, u32[]{:S(2)}) collective-permute-start(f32[512,384]{1,0:T(8,128)} %fusion.78), channel_id=1, source_target_pairs={{32,0},{36,4},{40,8},{44,12},{48,16},{52,20},{56,24},{60,28},{64,3... | collective-permute-start | bytes 2359304 | tf_op jit(solution)/shard_map/ppermute | solution.py:12
  558.4 25.4 %collective-permute-start.7 = (f32[512,384]{1,0:T(8,128)}, f32[512,384]{1,0:T(8,128)}, u32[]{:S(2)}, u32[]{:S(2)}) collective-permute-start(f32[512,384]{1,0:T(8,128)} %fusion.78), channel_id=1, source_target_pairs={{0,32},{4,36},{8,40},{12,44},{16,48},{20,52},{24,56},{28,60},{32,6... | collective-permute-start | bytes 2359304 | tf_op jit(solution)/shard_map/ppermute | solution.py:12
  586.9 64.2 %all-gather.46.cloned.1.call-start = ((), (), s32[]{:S(2)}) async-start(), calls=%async_computation.14 | async-start | bytes 1310720 | tf_op jit(solution)/shard_map/all_gather | solution.py:161
  590.3 78.7 %all-gather.42.cloned.1.call-start = ((), (), s32[]{:S(2)}) async-start(), calls=%async_computation.12 | async-start | bytes 1310720 | tf_op jit(solution)/shard_map/all_gather | solution.py:160
  593.3 105.1 %all-gather.48.cloned.1.call-start = ((), (), s32[]{:S(2)}) async-start(), calls=%async_computation.15 | async-start | bytes 1310720 | tf_op jit(solution)/shard_map/all_gather | solution.py:183
  642.3 20.8 %collective-permute-start.10 = (f32[512,384]{1,0:T(8,128)}, f32[512,384]{1,0:T(8,128)}, u32[]{:S(2)}, u32[]{:S(2)}) collective-permute-start(f32[512,384]{1,0:T(8,128)} %fusion.84), channel_id=1, source_target_pairs={{64,0},{68,4},{72,8},{76,12},{80,16},{84,20},{88,24},{92,28},{96,3... | collective-permute-start | bytes 2359304 | tf_op jit(solution)/shard_map/ppermute | solution.py:12
  643.6 25.5 %collective-permute-start.9 = (f32[512,384]{1,0:T(8,128)}, f32[512,384]{1,0:T(8,128)}, u32[]{:S(2)}, u32[]{:S(2)}) collective-permute-start(f32[512,384]{1,0:T(8,128)} %fusion.84), channel_id=1, source_target_pairs={{0,64},{4,68},{8,72},{12,76},{16,80},{20,84},{24,88},{28,92},{32,9... | collective-permute-start | bytes 2359304 | tf_op jit(solution)/shard_map/ppermute | solution.py:12
  725.8 8.3 %collective-permute-start.11 = (f32[512,128]{1,0:T(8,128)S(1)}, f32[512,128]{1,0:T(8,128)S(1)}, u32[]{:S(2)}, u32[]{:S(2)}) collective-permute-start(f32[512,128]{1,0:T(8,128)S(1)} %fusion.140), channel_id=1, source_target_pairs={{0,4},{4,8},{8,12},{12,16},{16,20},{20,24},{24,28},{28,32},{32,36}... | collective-permute-start | bytes 786440 | tf_op jit(solution)/shard_map/ppermute | solution.py:12
  (14 other events, 243.3 us)
Sparse Core Ops, SparseCore 0:
  24.5 27.4 all-gather.49
  82.4 26.3 all-gather.49
  139.1 26.3 all-gather.49
Sparse Core Ops, SparseCore 1:
  236.1 24.7 all-gather.19
  262.4 26.1 all-gather.21
  290.1 26.2 all-gather.17
  319.6 26.2 all-gather.25
  347.6 26.2 all-gather.27
  375.5 26.2 all-gather.23
  404.9 26.2 all-gather.31
  432.6 26.2 all-gather.33
  460.4 26.2 all-gather.29
  489.8 38.2 all-gather.37
  529.6 26.2 all-gather.39
  557.6 26.2 all-gather.35
  586.9 26.2 all-gather.43
  614.9 26.2 all-gather.45
  642.8 26.2 all-gather.41
  672.2 26.2 all-gather.47

commit v2 on v0

v2 whole, which is shorter than its diff:
```python
import functools
import jax
import jax.numpy as jnp
from jax import lax
from jax.experimental import pallas as pl
from jax.experimental.pallas import tpu as pltpu
from jax.sharding import PartitionSpec as P

W = 16
BF = jnp.bfloat16
F32 = jnp.float32


def invert_panel(lanes, block, k):
    first = W * k
    tiles = W // 8
    rows = jnp.concatenate(block[tiles * k : tiles * (k + 1)], axis=0)
    cols = [jnp.broadcast_to(rows[:, first + p : first + p + 1], (W, 128)) for p in range(W)]
    others = [i for i in range(16) if not tiles * k <= i < tiles * (k + 1)]
    wide = {
        i: [jnp.broadcast_to(block[i][:, first + p : first + p + 1], (8, 128)) for p in range(W)]
        for i in others
    }
    inside = (lanes >= first) & (lanes < first + W)
    sub = lax.broadcasted_iota(jnp.int32, (W, 128), 0)
    lane = lax.broadcasted_iota(jnp.int32, (W, 128), 1) - first
    rows = jnp.where((lane >= 0) & (lane < W), (lane == sub).astype(F32), rows)
    for p in range(W):
        pivot = 1.0 / cols[p][p : p + 1, :]
        here = sub == p
        scaled = rows[p : p + 1, :] * pivot
        rows = jnp.where(here, scaled, rows - cols[p] * scaled)
        for j in range(p + 1, W):
            scaled_j = cols[j][p : p + 1, :] * pivot
            cols[j] = jnp.where(here, scaled_j, cols[j] - cols[p] * scaled_j)
    out = [None] * 16
    for i in range(tiles):
        out[tiles * k + i] = rows[8 * i : 8 * i + 8]
    for i in others:
        acc = jnp.where(inside, 0.0, block[i])
        for p in range(W):
            acc = acc - wide[i][p] * rows[p : p + 1, :]
        out[i] = acc
    return out


def invert128(block):
    lanes = lax.broadcasted_iota(jnp.int32, (8, 128), 1)
    tiles = [block[8 * i : 8 * i + 8] for i in range(16)]
    for k in range(128 // W):
        tiles = invert_panel(lanes, tiles, k)
    return jnp.concatenate(tiles, axis=0)


def pieces(x):
    high = x.astype(BF)
    rest = x - high.astype(F32)
    mid = rest.astype(BF)
    low = (rest - mid.astype(F32)).astype(BF)
    return high, mid, low


def left6(x):
    h, m, l = pieces(x)
    return jnp.concatenate([h, m, h, m, h, l], axis=1)


def right6(x):
    h, m, l = pieces(x)
    return jnp.concatenate([h, h, m, m, l, h], axis=0)


def dot(a, b):
    return jnp.dot(a, b, preferred_element_type=F32)


def at(i, size):
    return pl.ds(pl.multiple_of(i * size, size), size)


def reduce_rows(m, u6, n_tiles):
    def step(j, c):
        s = at(j, 128)
        w6 = left6(invert128(m[s, s]))
        rowid = lax.broadcasted_iota(jnp.int32, (512, 1), 0) // 128
        u6[...] = left6(jnp.where(rowid == j, 0.0, m[:, s]))

        def tile(i, c):
            n = at(i, 256)
            t = dot(w6, right6(m[s, n]))
            t6 = right6(t)
            m[:, n] = m[:, n] - dot(u6[...], t6)
            m[s, n] = t
            return c

        lax.fori_loop((j + 1) // 2, n_tiles, tile, 0)
        return c

    lax.fori_loop(0, 4, step, 0)


def schur(et, g3, m, base, outs):
    ll, lr, rr, rl_, rr_ = outs
    b_ll, b_rr, b_rl_, b_rr_ = base
    parts = pieces(m[:, 512:1792])
    for q in range(3):
        g3[q] = parts[q]

    def term(i, n, cols=256):
        e = left6(et[at(i, 256), :])
        c = pl.ds(pl.multiple_of(n * 256, 256), cols)
        h, mm, l = g3[0, :, c], g3[1, :, c], g3[2, :, c]
        return dot(e, jnp.concatenate([h, h, mm, mm, l, h], axis=0))

    def body(q, c):
        i, n = q // 2, q % 2
        r, k = at(i, 256), at(n, 256)
        ll[r, k] = b_ll(r, k) - term(i, n)
        lr[r, k] = -term(i, n + 2)
        rr[r, k] = b_rr(r, k) - term(i + 2, n + 2)
        return c

    lax.fori_loop(0, 4, body, 0)

    def rhs(i, c):
        r = at(i, 256)
        rl_[r, :] = b_rl_(r) - term(i, 4, 128)
        rr_[r, :] = b_rr_(r) - term(i + 2, 4, 128)
        return c

    lax.fori_loop(0, 2, rhs, 0)


def fill(m, et, f):
    m[:, 1536:1664] = f
    m[:, 1664:1792] = jnp.zeros((512, 128), F32)


def first_kernel(p, x1, x2, f, d, fd, g, gf, ll, lr, rr, rl_, rr_, m, u6, et, g3):
    m[:, 0:512] = p[...]
    m[:, 512:1024] = x1[...]
    et[0:512, :] = x1[...].T
    et[512:1024, :] = x2[...]
    m[:, 1024:1536] = x2[...].T
    fill(m, et, f[...])
    reduce_rows(m, u6, 7)
    g[...] = m[:, 512:1536]
    gf[...] = m[:, 1536:1664]
    zero = lambda r, k=None: 0.0
    schur(et, g3, m, (zero, lambda r, k: d[r, k], zero, lambda r: fd[r, :]), (ll, lr, rr, rl_, rr_))


def merge_kernel(bit, all_, alr, arr, arl, arr_, bll, blr, brr, brl, brr_,
                 g, gf, ll, lr, rr, rl_, rr_, m, u6, et, g3):
    def load(own, other):
        oll, olr, orr, orl, orr_ = own
        pll, plr, prr, prl, prr_ = other
        m[:, 0:512] = orr[...] + pll[...]
        et[0:512, :] = olr[...]
        m[:, 1024:1536] = plr[...]
        ll[...] = oll[...]
        rr[...] = prr[...]
        rl_[...] = orl[...]
        rr_[...] = prr_[...]
        fill(m, et, orr_[...] + prl[...])

    mine = (all_, alr, arr, arl, arr_)
    other = (bll, blr, brr, brl, brr_)

    @pl.when(bit[0] == 0)
    def _():
        load(mine, other)

    @pl.when(bit[0] != 0)
    def _():
        load(other, mine)

    m[:, 512:1024] = et[0:512, :].T
    et[512:1024, :] = m[:, 1024:1536].T
    reduce_rows(m, u6, 7)
    g[...] = m[:, 512:1536]
    gf[...] = m[:, 1536:1664]
    schur(et, g3, m,
          (lambda r, k: ll[r, k], lambda r, k: rr[r, k], lambda r: rl_[r, :], lambda r: rr_[r, :]),
          (ll, lr, rr, rl_, rr_))


def last_kernel(p, f, x, m, u6):
    m[:, 0:512] = p[...]
    m[:, 512:640] = f[...]
    m[:, 640:768] = jnp.zeros((512, 128), F32)
    reduce_rows(m, u6, 3)
    x[...] = m[:, 512:640]


def vm(n):
    return [pl.BlockSpec(memory_space=pltpu.VMEM)] * n


def shapes(*dims):
    return tuple(jax.ShapeDtypeStruct(d, F32) for d in dims)


SQ, TH = (512, 512), (512, 128)
STATE = (SQ, SQ, SQ, TH, TH)
PARAMS = pltpu.CompilerParams(vmem_limit_bytes=44 * 2**20)
COST = pl.CostEstimate(flops=18 * 10**9, bytes_accessed=2**24, transcendentals=0)
WORK = [
    pltpu.VMEM((512, 1792), F32),
    pltpu.VMEM((512, 768), BF),
    pltpu.VMEM((1024, 512), F32),
    pltpu.VMEM((3, 512, 1280), BF),
]


def eliminate(p, x1, x2, f, d, fd):
    out = pl.pallas_call(
        first_kernel, out_shape=shapes((512, 1024), TH, *STATE), in_specs=vm(6), out_specs=vm(7),
        scratch_shapes=WORK, compiler_params=PARAMS, cost_estimate=COST,
    )(p, x1, x2, f, d, fd)
    return out[:2], out[2:]


def merge(bit, mine, other):
    out = pl.pallas_call(
        merge_kernel, out_shape=shapes((512, 1024), TH, *STATE),
        in_specs=[pl.BlockSpec(memory_space=pltpu.SMEM)] + vm(10), out_specs=vm(7),
        scratch_shapes=WORK, compiler_params=PARAMS, cost_estimate=COST,
    )(bit, *mine, *other)
    return out[:2], out[2:]


def finish(p, f):
    return pl.pallas_call(
        last_kernel, out_shape=shapes(TH)[0], in_specs=vm(2), out_specs=vm(1)[0],
        scratch_shapes=[pltpu.VMEM((512, 768), F32), WORK[1]], compiler_params=PARAMS, cost_estimate=COST,
    )(p, f)


MESH_ID = pl.DeviceIdType.MESH


def partner_of(seg, level):
    if level == 0:
        return seg + 1 - 2 * lax.rem(seg, 2)
    core, x, y = lax.rem(seg, 2), lax.rem(lax.div(seg, 2), 4), lax.div(seg, 8)
    if level == 1:
        x = x + 1 - 2 * lax.rem(x, 2)
    if level == 2:
        x = 3 - x
    if level == 3:
        y = y + 1 - 2 * lax.rem(y, 2)
    if level == 4:
        y = 3 - y
    return (y * 4 + x) * 2 + core


def exchange_kernel(level, m, r, pm, pr, sx, rx, sz, rz, sd, rd):
    seg, col = lax.axis_index("seg"), lax.axis_index("col")
    core = lax.rem(seg, 2)
    sibling = partner_of(seg, 0)
    partner = partner_of(seg, level)
    barrier = pltpu.get_barrier_semaphore()
    peers = [(sibling, col)]
    if level > 0:
        peers += [(partner, col)] + [(seg, lax.rem(col + d, 4)) for d in (1, 2, 3)]
    for peer in peers:
        pl.semaphore_signal(barrier, inc=1, device_id=peer, device_id_type=MESH_ID)
    pl.semaphore_wait(barrier, len(peers))

    def copy(src, dst, s, d, peer):
        return pltpu.make_async_remote_copy(
            src_ref=src, dst_ref=dst, send_sem=s, recv_sem=d, device_id=peer, device_id_type=MESH_ID
        )

    if level == 0:
        copies = [
            copy(m, pm, sx.at[0], rx.at[0], (partner, col)),
            copy(r, pr, sx.at[1], rx.at[1], (partner, col)),
        ]
        for c in copies:
            c.start()
        for c in copies:
            c.wait()
        return
    rows = 1536 // 8 // CHUNKS

    def part(owner, k):
        return pl.ds(pl.multiple_of((owner * CHUNKS + k) * rows, rows), rows)

    mine = col * 2 + core
    across = []
    for k in range(CHUNKS):
        c = copy(m.at[part(mine, k)], pm.at[part(mine, k)], sx.at[k], rx.at[k], (partner, col))
        c.start()
        across.append(c)
    half = pl.ds(pl.multiple_of(core * 512, 512), 512)
    rhs = copy(r.at[half], pr.at[half], sx.at[CHUNKS], rx.at[CHUNKS], (partner, col))
    rhs.start()
    onward, beside = [], []
    for k in range(CHUNKS):
        across[k].wait_recv()
        piece = pm.at[part(mine, k)]
        for d in (1, 3, 2):
            c = copy(piece, piece, sz.at[d - 1, k], rz.at[d - 1, k], (seg, lax.rem(col + d, 4)))
            c.start()
            onward.append((d, k, c))
        c = copy(piece, piece, sd.at[0, k], rd.at[0, k], (sibling, col))
        c.start()
        beside.append(c)
    rhs.wait_recv()
    c = copy(pr.at[half], pr.at[half], sx.at[CHUNKS + 1], rx.at[CHUNKS + 1], (sibling, col))
    c.start()
    beside.append(c)
    for d, k, c in onward:
        c.wait_recv()
        owner = lax.rem(col + 4 - d, 4) * 2 + core
        piece = pm.at[part(owner, k)]
        c = copy(piece, piece, sd.at[d, k], rd.at[d, k], (sibling, col))
        c.start()
        beside.append(c)
    for c in beside:
        c.wait_recv()
    for c in across + [rhs] + [c for _, _, c in onward] + beside:
        c.wait_send()


CHUNKS = 3


def exchange(m, r, level):
    dma = pltpu.SemaphoreType.DMA
    return pl.pallas_call(
        functools.partial(exchange_kernel, level),
        out_shape=shapes(m.shape, r.shape),
        in_specs=[pl.BlockSpec(memory_space=pl.ANY)] * 2,
        out_specs=[pl.BlockSpec(memory_space=pl.ANY)] * 2,
        scratch_shapes=[
            dma((CHUNKS + 2,)), dma((CHUNKS + 2,)), dma((3, CHUNKS)), dma((3, CHUNKS)),
            dma((4, CHUNKS)), dma((4, CHUNKS)),
        ],
        compiler_params=pltpu.CompilerParams(collective_id=level, has_side_effects=True),
    )(m, r)


def all_columns(blocks):
    share = blocks.shape[2]
    around = [blocks]
    for d in (1, 2, 3):
        pairs = [(i, (i - d) % 4) for i in range(4)]
        around.append(lax.ppermute(blocks, "col", pairs))
    twice = jnp.concatenate(around + around[:3], axis=2)
    first = lax.rem(4 - lax.axis_index("col"), 4) * share
    return lax.dynamic_slice_in_dim(twice, first, 4 * share, 2)


def product(a, b):
    return jnp.dot(a, b, precision=lax.Precision.HIGHEST, preferred_element_type=F32)


def on_device(diagonal, lower, right_side):
    size = lower.shape[1]
    seg = lax.axis_index("seg")
    even = all_columns(jnp.stack([diagonal[0], diagonal[2]]))
    odd = all_columns(jnp.stack([diagonal[1], diagonal[3]]))
    left = lower[0] * (seg > 0).astype(F32)
    saved = []
    kept, low = eliminate(even[0], left, lower[1], right_side[0], odd[0], right_side[1])
    saved.append(kept)
    kept, high = eliminate(even[1], lower[2], lower[3], right_side[2], odd[1], right_side[3])
    saved.append(kept)
    kept, state = merge(jnp.zeros((1,), jnp.int32), low, high)
    saved.append(kept)
    for level in range(5):
        ll, lr, rr, rl_, rr_ = state
        m, r = exchange(jnp.concatenate([ll, lr, rr], axis=0), jnp.concatenate([rl_, rr_], axis=0), level)
        other = (m[:size], m[size : 2 * size], m[2 * size :], r[:size], r[size:])
        bit = lax.rem(lax.div(seg, 2**level), 2)
        kept, state = merge(bit.reshape(1).astype(jnp.int32), state, other)
        saved.append(kept)
    right = finish(state[2], state[4])
    lefts = jnp.zeros_like(right)

    def between(kept, a, b):
        g, gf = kept
        return gf - product(g, jnp.concatenate([a, b], axis=0))

    for level in range(4, -1, -1):
        middle = between(saved[3 + level], lefts, right)
        bit = lax.rem(lax.div(seg, 2**level), 2)
        lefts, right = jnp.where(bit == 0, lefts, middle), jnp.where(bit == 0, middle, right)
    second = between(saved[2], lefts, right)
    return jnp.stack([between(saved[0], lefts, second), second, between(saved[1], second, right), right])


def solution(mesh):
    in_specs = (P("seg", None, "col"), P("seg", None, None), P("seg", None, "col"))
    return jax.shard_map(
        on_device, mesh=mesh, in_specs=in_specs, out_specs=P("seg", None, "col"), check_vma=False
    )
```

time: 1970 us -> 615 us (0.31)
  other arithmetic: 1140 us -> 22.3 us
  Pallas kernels: 0 us -> 488 us
  matrix products: 331 us -> 14.6 us
  waiting for transfers between devices: 226 us -> 29.4 us
  local copies, waits for them, and re-layouts: 169 us -> 46.1 us
  starting transfers between devices: 49.7 us -> 9.01 us
  between operations: 32.2 us -> 1.05 us
    another operation x156 -> x4, other arithmetic: 1100 us -> 3.37 us  [the longest x1 1.18 us: on_device(): odd = all_columns(jnp.stack([diagonal[1], diagonal[3]]))]
    pallas_call x0 -> x14, Pallas kernels: none -> 488 us  [the longest x6 260 us: merge(): pl.pallas_call(merge_kernel, out_shape=shapes((512, 1024), TH, *STATE), i...]
    dot_general x77 -> x8, matrix products: 210 us -> 14.6 us  [product(): jnp.dot(a, b, precision=lax.Precision.HIGHEST, preferred_element_type=F32)]
    all_gather x19 -> x0, waiting for transfers between devices: 165 us -> none  [the longest x5 95.3 us: on_device(): lax.all_gather(pivot_block, 'col', axis=1, tiled=True)]
    another operation x117 -> x0, matrix products: 121 us -> none  [the longest x63 66 us: invert_spd(): lax.linalg.triangular_solve(factor, identity, left_side=True, lower=True)]
    another operation x160 -> x0, local copies, waits for them, and re-layouts: 118 us -> none  [the longest x118 105 us: invert_spd(): lax.linalg.triangular_solve(factor, identity, left_side=True, lower=True)]
    ppermute x12 -> x6, starting transfers between devices: 47.3 us -> 9.01 us  [all_columns(): around.append(lax.ppermute(blocks, 'col', pairs))]
    ppermute x12 -> x6, waiting for transfers between devices: 59.6 us -> 29.4 us  [all_columns(): around.append(lax.ppermute(blocks, 'col', pairs))]
  transfers between devices with their start and end apart: 31 -> 6, of which waited for: 16 -> 4; matrix products, arithmetic and copies ran while one was open for 46% -> 2% of each run, Pallas kernels for 0% -> 0%
where the time goes in v2:
time: 615 us; the launch traced here: 611 us
  Pallas kernels  488 us (79%)
  local copies, waits for them, and re-layouts  46.1 us (7%)
  waiting for transfers between devices  29.4 us (5%)
  other arithmetic  22.3 us (4%)
  matrix products  14.6 us (2%)
  starting transfers between devices  9.01 us (1%)
    pallas_call x6, Pallas kernels, merge(): pl.pallas_call(merge_kernel, out_shape=shapes((512, 1024), TH, *STATE), i...  260 us
    pallas_call x5, Pallas kernels, exchange(): pl.pallas_call(functools.partial(exchange_kernel, level), out_shape=shape...  123 us
    pallas_call x2, Pallas kernels, eliminate(): pl.pallas_call(first_kernel, out_shape=shapes((512, 1024), TH, *STATE), i...  83.7 us
    ppermute x6, waiting for transfers between devices, all_columns(): around.append(lax.ppermute(blocks, 'col', pairs))  29.4 us
    unnamed x154, local copies, waits for them, and re-layouts  24.7 us
    pallas_call x1, Pallas kernels, finish(): pl.pallas_call(last_kernel, out_shape=shapes(TH)[0], in_specs=vm(2), out_...  21.5 us
    slice x10, local copies, waits for them, and re-layouts, on_device(): other = (m[:size], m[size:2 * size], m[2 * size:], r[:size], r[size:])  16.5 us
    dot_general x8, matrix products, product(): jnp.dot(a, b, precision=lax.Precision.HIGHEST, preferred_element_type=F32)  14.6 us
  transfers between devices with their start and end apart: 6, of which 4 were waited for; matrix products, arithmetic and copies ran while one was open for 2% of the time, Pallas kernels for 0%

profile of v2, /device:TPU:1, one launch (start us, length us, event | category | flops | bytes accessed | tf_op | source)
XLA Modules:
  0.0 610.8 jit_solution(17538580002915916525)
XLA Ops:
  2.5 4.6 collective-permute-start.3
  8.9 2.0 collective-permute-start
  12.6 3.9 slice_bitcast_fusion
  17.4 11.6 %collective-permute-done.3 = f32[2,512,128]{2,1,0:T(8,128)} collective-permute-done((f32[2,512,128]{2,1,0:T(8,128)}, f32[2,512,128]{2,1,0:T(8,128)}, u32[]{:S(2)}, u32[]{:S(2)}) %collective-permute-start.3) | collective-permute-done | bytes 524320 | tf_op jit(solution)/shard_map/ppermute | solution.py:351
  31.0 2.0 constant_dynamic-update-slice_fusion.11
  36.8 14.7 %collective-permute-done = f32[2,512,128]{2,1,0:T(8,128)} collective-permute-done((f32[2,512,128]{2,1,0:T(8,128)}, f32[2,512,128]{2,1,0:T(8,128)}, u32[]{:S(2)}, u32[]{:S(2)}) %collective-permute-start) | collective-permute-done | bytes 524320 | tf_op jit(solution)/shard_map/ppermute | solution.py:351
  53.7 2.0 collective-permute-done.2
  60.9 41.8 %shard_map.38 = (f32[512,1024]{1,0:T(8,128)}, f32[512,128]{1,0:T(8,128)S(1)}, f32[512,512]{1,0:T(8,128)S(1)}, f32[512,512]{1,0:T(8,128)S(1)}, f32[512,512]{1,0:T...) custom-call(f32[512,512]{1,0:T(8,128)S(1)} %get-tuple-element.137.p, f32[512,512]{1,0:T(8,128)S(1)} %copy-done, ...), custom_call_target="tpu_custom_call" | custom-call | flops 17999998976 | bytes 16777216 | tf_op jit(solution)/shard_map/pallas_call | solution.py:217
  104.4 41.9 %shard_map.37 = (f32[512,1024]{1,0:T(8,128)}, f32[512,128]{1,0:T(8,128)S(1)}, f32[512,512]{1,0:T(8,128)S(1)}, f32[512,512]{1,0:T(8,128)S(1)}, f32[512,512]{1,0:T...) custom-call(f32[512,512]{1,0:T(8,128)S(1)} %get-tuple-element.138.p, f32[512,512]{1,0:T(8,128)S(1)} %get-tuple-element.133.x1, ...), custom_call_target="tpu_custom_call" | custom-call | flops 17999998976 | bytes 16777216 | tf_op jit(solution)/shard_map/pallas_call | solution.py:217
  147.0 43.0 %shard_map.39 = (f32[512,1024]{1,0:T(8,128)}, f32[512,128]{1,0:T(8,128)S(1)}, f32[512,512]{1,0:T(8,128)S(1)}, f32[512,512]{1,0:T(8,128)S(1)}, f32[512,512]{1,0:T...) custom-call(s32[1]{0:T(128)} %constant.47.clone.1.bit, f32[512,512]{1,0:T(8,128)S(1)} %get-tuple-element.70.all_, ...), custom_call_target="tpu_custom_call" | custom-call | flops 17999998976 | bytes 16777216 | tf_op jit(solution)/shard_map/pallas_call | solution.py:225
  191.6 1.9 pad_maximum_fusion.m
  193.5 7.7 %shard_map.40 = (f32[1536,512]{1,0:T(8,128)}, f32[1024,128]{1,0:T(8,128)}) custom-call(f32[1536,512]{1,0:T(8,128)} %pad_maximum_fusion.m, f32[1024,128]{1,0:T(8,128)} %pad_maximum_fusion.14.r), custom_call_target="tpu_custom_call" | custom-call | tf_op jit(solution)/shard_map/pallas_call | solution.py:333
  201.2 3.2 fusion.29
  204.5 43.1 %shard_map.41 = (f32[512,1024]{1,0:T(8,128)}, f32[512,128]{1,0:T(8,128)S(1)}, f32[512,512]{1,0:T(8,128)S(1)}, f32[512,512]{1,0:T(8,128)S(1)}, f32[512,512]{1,0:T...) custom-call(s32[1]{0:T(128)} %bitcast.10.bit, f32[512,512]{1,0:T(8,128)S(1)} %get-tuple-element.80.all_, ...), custom_call_target="tpu_custom_call" | custom-call | flops 17999998976 | bytes 16777216 | tf_op jit(solution)/shard_map/pallas_call | solution.py:225
  250.6 1.9 pad_maximum_fusion.1.m
  254.6 28.8 %shard_map.42 = (f32[1536,512]{1,0:T(8,128)}, f32[1024,128]{1,0:T(8,128)}) custom-call(f32[1536,512]{1,0:T(8,128)} %pad_maximum_fusion.1.m, f32[1024,128]{1,0:T(8,128)} %pad_maximum_fusion.15.r), custom_call_target="tpu_custom_call" | custom-call | tf_op jit(solution)/shard_map/pallas_call | solution.py:333
  283.4 3.3 fusion.28
  286.8 43.2 %shard_map.43 = (f32[512,1024]{1,0:T(8,128)}, f32[512,128]{1,0:T(8,128)S(1)}, f32[512,512]{1,0:T(8,128)S(1)}, f32[512,512]{1,0:T(8,128)S(1)}, f32[512,512]{1,0:T...) custom-call(s32[1]{0:T(128)} %bitcast.9.bit, f32[512,512]{1,0:T(8,128)S(1)} %copy-done.2, ...), custom_call_target="tpu_custom_call" | custom-call | flops 17999998976 | bytes 16777216 | tf_op jit(solution)/shard_map/pallas_call | solution.py:225
  332.3 1.9 pad_maximum_fusion.2.m
  334.3 29.1 %shard_map.44 = (f32[1536,512]{1,0:T(8,128)}, f32[1024,128]{1,0:T(8,128)}) custom-call(f32[1536,512]{1,0:T(8,128)} %pad_maximum_fusion.2.m, f32[1024,128]{1,0:T(8,128)} %pad_maximum_fusion.16.r), custom_call_target="tpu_custom_call" | custom-call | tf_op jit(solution)/shard_map/pallas_call | solution.py:333
  363.5 3.2 fusion.27
  366.7 43.4 %shard_map.45 = (f32[512,1024]{1,0:T(8,128)}, f32[512,128]{1,0:T(8,128)S(1)}, f32[512,512]{1,0:T(8,128)S(1)}, f32[512,512]{1,0:T(8,128)S(1)}, f32[512,512]{1,0:T...) custom-call(s32[1]{0:T(128)} %bitcast.8.bit, f32[512,512]{1,0:T(8,128)S(1)} %get-tuple-element.94.all_, ...), custom_call_target="tpu_custom_call" | custom-call | flops 17999998976 | bytes 16777216 | tf_op jit(solution)/shard_map/pallas_call | solution.py:225
  413.2 1.9 pad_maximum_fusion.3.m
  417.1 28.6 %shard_map.46 = (f32[1536,512]{1,0:T(8,128)}, f32[1024,128]{1,0:T(8,128)}) custom-call(f32[1536,512]{1,0:T(8,128)} %pad_maximum_fusion.3.m, f32[1024,128]{1,0:T(8,128)} %pad_maximum_fusion.17.r), custom_call_target="tpu_custom_call" | custom-call | tf_op jit(solution)/shard_map/pallas_call | solution.py:333
  445.7 3.3 fusion.26
  449.2 43.2 %shard_map.47 = (f32[512,1024]{1,0:T(8,128)}, f32[512,128]{1,0:T(8,128)S(1)}, f32[512,512]{1,0:T(8,128)S(1)}, f32[512,512]{1,0:T(8,128)S(1)}, f32[512,512]{1,0:T...) custom-call(s32[1]{0:T(128)} %bitcast.7.bit, f32[512,512]{1,0:T(8,128)S(1)} %copy-done.8, ...), custom_call_target="tpu_custom_call" | custom-call | flops 17999998976 | bytes 16777216 | tf_op jit(solution)/shard_map/pallas_call | solution.py:225
  494.6 1.9 pad_maximum_fusion.4.m
  496.6 29.2 %shard_map.48 = (f32[1536,512]{1,0:T(8,128)}, f32[1024,128]{1,0:T(8,128)}) custom-call(f32[1536,512]{1,0:T(8,128)} %pad_maximum_fusion.4.m, f32[1024,128]{1,0:T(8,128)} %pad_maximum_fusion.18.r), custom_call_target="tpu_custom_call" | custom-call | tf_op jit(solution)/shard_map/pallas_call | solution.py:333
  525.8 3.2 fusion.25
  529.1 44.0 %shard_map.49 = (f32[512,1024]{1,0:T(8,128)}, f32[512,128]{1,0:T(8,128)S(1)}, f32[512,512]{1,0:T(8,128)}, f32[512,512]{1,0:T(8,128)}, f32[512,512]{1,0:T(8,128)S...) custom-call(s32[1]{0:T(128)} %bitcast.6.bit, f32[512,512]{1,0:T(8,128)S(1)} %get-tuple-element.108.all_, ...), custom_call_target="tpu_custom_call" | custom-call | flops 17999998976 | bytes 16777216 | tf_op jit(solution)/shard_map/pallas_call | solution.py:225
  573.0 21.5 %shard_map.50 = f32[512,128]{1,0:T(8,128)S(1)} custom-call(f32[512,512]{1,0:T(8,128)S(1)} %get-tuple-element.117.p, f32[512,128]{1,0:T(8,128)S(1)} %get-tuple-element.118.f), custom_call_target="tpu_custom_call" | custom-call | flops 17999998976 | bytes 16777216 | tf_op jit(solution)/shard_map/pallas_call | solution.py:234
  605.7 2.0 fusion
  (189 shorter events, 52.6 us)
Async XLA Ops:
  1.3 6.5 %copy-start.49 = (f32[1,512,128]{2,1,0:T(8,128)}, f32[1,512,128]{2,1,0:T(8,128)S(1)}, u32[]{:S(2)}) copy-start(f32[1,512,128]{2,1,0:T(8,128)S(1)} %get-tuple-element.159) | copy-start | bytes 786436
  1.3 7.6 %copy-start.51 = (f32[1,512,128]{2,1,0:T(8,128)}, f32[1,512,128]{2,1,0:T(8,128)S(1)}, u32[]{:S(2)}) copy-start(f32[1,512,128]{2,1,0:T(8,128)S(1)} %get-tuple-element.160) | copy-start | bytes 786436
  1.3 7.6 %copy-start.53 = (f32[1,512,128]{2,1,0:T(8,128)}, f32[1,512,128]{2,1,0:T(8,128)S(1)}, u32[]{:S(2)}) copy-start(f32[1,512,128]{2,1,0:T(8,128)S(1)} %get-tuple-element.158) | copy-start | bytes 786436
  1.3 9.5 %copy-start.55 = (f32[1,512,128]{2,1,0:T(8,128)}, f32[1,512,128]{2,1,0:T(8,128)S(1)}, u32[]{:S(2)}) copy-start(f32[1,512,128]{2,1,0:T(8,128)S(1)} %get-tuple-element.161) | copy-start | bytes 786436
  2.5 26.6 %collective-permute-start.3 = (f32[2,512,128]{2,1,0:T(8,128)}, f32[2,512,128]{2,1,0:T(8,128)}, u32[]{:S(2)}, u32[]{:S(2)}) collective-permute-start(f32[2,512,128]{2,1,0:T(8,128)} %get-tuple-element.172), channel_id=1, source_target_pairs={{0,3},{1,0},{2,1},{3,2},{4,7},{5,4},{6,5},{7,6},{8,11},{9,8},{10,9... | collective-permute-start | bytes 1572872 | tf_op jit(solution)/shard_map/ppermute | solution.py:351
  7.1 23.9 %collective-permute-start.4 = (f32[2,512,128]{2,1,0:T(8,128)}, f32[2,512,128]{2,1,0:T(8,128)}, u32[]{:S(2)}, u32[]{:S(2)}) collective-permute-start(f32[2,512,128]{2,1,0:T(8,128)} %get-tuple-element.172), channel_id=1, source_target_pairs={{0,2},{1,3},{2,0},{3,1},{4,6},{5,7},{6,4},{7,5},{8,10},{9,11},{10,... | collective-permute-start | bytes 1572872 | tf_op jit(solution)/shard_map/ppermute | solution.py:351
  7.1 27.0 %collective-permute-start.5 = (f32[2,512,128]{2,1,0:T(8,128)}, f32[2,512,128]{2,1,0:T(8,128)}, u32[]{:S(2)}, u32[]{:S(2)}) collective-permute-start(f32[2,512,128]{2,1,0:T(8,128)} %get-tuple-element.172), channel_id=1, source_target_pairs={{0,1},{1,2},{2,3},{3,0},{4,5},{5,6},{6,7},{7,4},{8,9},{9,10},{10,1... | collective-permute-start | bytes 1572872 | tf_op jit(solution)/shard_map/ppermute | solution.py:351
  8.9 42.7 %collective-permute-start = (f32[2,512,128]{2,1,0:T(8,128)}, f32[2,512,128]{2,1,0:T(8,128)}, u32[]{:S(2)}, u32[]{:S(2)}) collective-permute-start(f32[2,512,128]{2,1,0:T(8,128)} %get-tuple-element.174), channel_id=1, source_target_pairs={{0,3},{1,0},{2,1},{3,2},{4,7},{5,4},{6,5},{7,6},{8,11},{9,8},{10,9... | collective-permute-start | bytes 1572872 | tf_op jit(solution)/shard_map/ppermute | solution.py:351
  10.8 41.8 %collective-permute-start.1 = (f32[2,512,128]{2,1,0:T(8,128)}, f32[2,512,128]{2,1,0:T(8,128)}, u32[]{:S(2)}, u32[]{:S(2)}) collective-permute-start(f32[2,512,128]{2,1,0:T(8,128)} %get-tuple-element.174), channel_id=1, source_target_pairs={{0,2},{1,3},{2,0},{3,1},{4,6},{5,7},{6,4},{7,5},{8,10},{9,11},{10,... | collective-permute-start | bytes 1572872 | tf_op jit(solution)/shard_map/ppermute | solution.py:351
  12.6 3.9 copy-start.67
  17.4 18.5 %copy-start.54 = (f32[1,512,128]{2,1,0:T(8,128)S(1)}, f32[1,512,128]{2,1,0:T(8,128)}, u32[]{:S(2)}) copy-start(f32[1,512,128]{2,1,0:T(8,128)} %copy-done.53) | copy-start | bytes 786436
  17.4 18.5 %copy-start.56 = (f32[1,512,128]{2,1,0:T(8,128)S(1)}, f32[1,512,128]{2,1,0:T(8,128)}, u32[]{:S(2)}) copy-start(f32[1,512,128]{2,1,0:T(8,128)} %copy-done.55) | copy-start | bytes 786436
  17.4 34.1 %copy-start.65 = (f32[2,512,896]{2,1,0:T(8,128)S(1)}, f32[2,512,896]{2,1,0:T(8,128)}, u32[]{:S(2)}) copy-start(f32[2,512,896]{2,1,0:T(8,128)} %get-tuple-element.175) | copy-start | bytes 11010052
  29.1 26.6 %collective-permute-start.2 = (f32[2,512,128]{2,1,0:T(8,128)}, f32[2,512,128]{2,1,0:T(8,128)S(1)}, u32[]{:S(2)}, u32[]{:S(2)}) collective-permute-start(f32[2,512,128]{2,1,0:T(8,128)} %get-tuple-element.174), channel_id=1, source_target_pairs={{0,1},{1,2},{2,3},{3,0},{4,5},{5,6},{6,7},{7,4},{8,9},{9,10},{10,1... | collective-permute-start | bytes 1572872 | tf_op jit(solution)/shard_map/ppermute | solution.py:351
  31.0 24.8 %copy-start.50 = (f32[1,512,128]{2,1,0:T(8,128)S(1)}, f32[1,512,128]{2,1,0:T(8,128)}, u32[]{:S(2)}) copy-start(f32[1,512,128]{2,1,0:T(8,128)} %copy-done.49) | copy-start | bytes 786436
  31.0 24.8 %copy-start.52 = (f32[1,512,128]{2,1,0:T(8,128)S(1)}, f32[1,512,128]{2,1,0:T(8,128)}, u32[]{:S(2)}) copy-start(f32[1,512,128]{2,1,0:T(8,128)} %copy-done.51) | copy-start | bytes 786436
  36.8 19.0 %copy-start.66 = (f32[2,512,896]{2,1,0:T(8,128)S(1)}, f32[2,512,896]{2,1,0:T(8,128)}, u32[]{:S(2)}) copy-start(f32[2,512,896]{2,1,0:T(8,128)} %constant_dynamic-update-slice_fusion.9) | copy-start | bytes 11010052
  60.9 43.5 %copy-start.45 = (f32[512,128]{1,0:T(8,128)S(1)}, f32[512,128]{1,0:T(8,128)}, u32[]{:S(2)}) copy-start(f32[512,128]{1,0:T(8,128)} %get-tuple-element.156.f) | copy-start | bytes 786436
  283.4 3.4 copy-start.2
  445.7 3.4 copy-start.8
  573.0 21.5 %copy-start.64 = (f32[512,1024]{1,0:T(8,128)S(1)}, f32[512,1024]{1,0:T(8,128)}, u32[]{:S(2)}) copy-start(f32[512,1024]{1,0:T(8,128)} %get-tuple-element.116) | copy-start | bytes 6291460
  594.6 3.7 copy-start.18
  594.6 3.7 copy-start.62
  596.4 3.7 copy-start.16
  596.4 3.7 copy-start.61
  598.3 3.7 copy-start.14
  598.3 3.7 copy-start.60
  600.2 3.7 copy-start.57
  602.0 3.7 copy-start.59
  603.8 3.9 copy-start.58
  605.6 3.8 copy-start.22
  605.6 3.8 copy-start.24
  (47 other events, 96.5 us)

commit v3 on v0

v3 whole, which is shorter than its diff:
```python
import functools
import jax
import jax.numpy as jnp
from jax import lax
from jax.experimental import pallas as pl
from jax.experimental.pallas import tpu as pltpu
from jax.sharding import PartitionSpec as P

W = 16
BF = jnp.bfloat16
F32 = jnp.float32


def pieces(x):
    high = x.astype(BF)
    rest = x - high.astype(F32)
    mid = rest.astype(BF)
    low = (rest - mid.astype(F32)).astype(BF)
    return high, mid, low


def beside(h, m, l):
    return jnp.concatenate([h, m, h, m, h, l], axis=1)


def below(h, m, l):
    return jnp.concatenate([h, h, m, m, l, h], axis=0)


def dot(a, b):
    return jnp.dot(a, b, preferred_element_type=F32)


def at(i, size):
    return pl.ds(pl.multiple_of(i * size, size), size)


def invert128(block):
    sub = lax.broadcasted_iota(jnp.int32, (W, 128), 0)
    lane = lax.broadcasted_iota(jnp.int32, (W, 128), 1)
    count = 128 // W
    panels = [block[W * i : W * i + W] for i in range(count)]
    for k in range(count):
        first = W * k
        rows = panels[k]
        cols = [jnp.broadcast_to(rows[:, first + p : first + p + 1], (W, 128)) for p in range(W)]
        inside = (lane >= first) & (lane < first + W)
        after = k + 1 if k + 1 < count else None
        if after is not None:
            wide = [
                jnp.broadcast_to(panels[after][:, first + p : first + p + 1], (W, 128)) for p in range(W)
            ]
        rest = [i for i in range(count) if i not in (k, after)]
        left = beside(*pieces(jnp.concatenate([panels[i] for i in rest], axis=0)))
        rows = jnp.where(inside, (lane - first == sub).astype(F32), rows)
        diag = cols[0][0:1, :]
        for p in range(W):
            pivot = 1.0 / diag
            here = sub == p
            column = cols[p]
            for j in range(p + 1, W):
                if j == p + 1:
                    moved = cols[j] - (column * cols[j][p : p + 1, :]) * pivot
                    diag = moved[j : j + 1, :]
                    cols[j] = jnp.where(here, cols[j][p : p + 1, :] * pivot, moved)
                else:
                    scaled = cols[j][p : p + 1, :] * pivot
                    cols[j] = jnp.where(here, scaled, cols[j] - column * scaled)
            scaled = rows[p : p + 1, :] * pivot
            rows = jnp.where(here, scaled, rows - column * scaled)
        if after is not None:
            acc = jnp.where(inside, 0.0, panels[after])
            for p in range(W):
                acc = acc - wide[p] * rows[p : p + 1, :]
        padded = [
            jnp.concatenate(
                [jnp.zeros((first, 128), BF)] * (first > 0)
                + [q]
                + [jnp.zeros((112 - first, 128), BF)] * (first < 112),
                axis=0,
            )
            for q in pieces(rows)
        ]
        delta = dot(left, below(*padded))
        for n, i in enumerate(rest):
            panels[i] = jnp.where(inside, 0.0, panels[i]) - delta[W * n : W * n + W]
        panels[k] = rows
        if after is not None:
            panels[after] = acc
    return jnp.concatenate(panels, axis=0)


MESH_ID = pl.DeviceIdType.MESH


def partner_of(seg, level):
    if level == 0:
        return seg + 1 - 2 * lax.rem(seg, 2)
    core, x, y = lax.rem(seg, 2), lax.rem(lax.div(seg, 2), 4), lax.div(seg, 8)
    if level == 1:
        x = x + 1 - 2 * lax.rem(x, 2)
    if level == 2:
        x = 3 - x
    if level == 3:
        y = y + 1 - 2 * lax.rem(y, 2)
    if level == 4:
        y = 3 - y
    return (y * 4 + x) * 2 + core


def invert(p, hook):
    def step(j, c):
        hook(j)
        s = at(j, 128)
        w = invert128(p[s, s])
        rowid = lax.broadcasted_iota(jnp.int32, (512, 1), 0) // 128
        u6 = beside(*pieces(jnp.where(rowid == j, 0.0, p[:, s])))
        w6 = beside(*pieces(w))
        t = dot(w6, below(*pieces(p[s, :])))
        here = lax.broadcasted_iota(jnp.int32, (1, 512), 1) // 128 == j
        t = jnp.where(here, jnp.concatenate([w] * 4, axis=1), t)
        for n in (slice(0, 256), slice(256, 512)):
            p[:, n] = jnp.where(here[:, n], 0.0, p[:, n]) - dot(u6, below(*pieces(t[:, n])))
        p[s, :] = t
        return c

    lax.fori_loop(0, 4, step, 0)


def kernel(
    diag, low, right, x,
    dv, lv, rv, st, rh, p, p3, e, f, et, gg, gl, gf, fp, xs, keep,
    load_sem, ds, dr, xsend, xrecv, zsend, zrecv, csend, crecv, ready,
):
    seg, col = lax.axis_index("seg"), lax.axis_index("col")
    core = lax.rem(seg, 2)
    me = col * 2 + core
    sibling = (partner_of(seg, 0), col)
    around = [(seg, lax.rem(col + d, 4)) for d in (1, 2, 3)]
    across = [(partner_of(seg, level), col) for level in range(1, 5)]

    def remote(src, dst, s, d, peer):
        return pltpu.make_async_remote_copy(
            src_ref=src, dst_ref=dst, send_sem=s, recv_sem=d, device_id=peer, device_id_type=MESH_ID
        )

    columns = pl.ds(pl.multiple_of(col * 128, 128), 128)
    loads = [pltpu.make_async_copy(low.at[b], lv.at[b], load_sem.at[b]) for b in range(4)]
    loads.append(pltpu.make_async_copy(right, rv, load_sem.at[4]))
    own = [pltpu.make_async_copy(diag.at[b], dv.at[b, :, columns], load_sem.at[5 + b]) for b in range(4)]
    for c in [own[0], loads[0], loads[1], loads[4], own[2], loads[2], loads[3], own[1], own[3]]:
        c.start()
    barrier = pltpu.get_barrier_semaphore()
    for peer in [sibling] + around + across:
        pl.semaphore_signal(barrier, inc=1, device_id=peer, device_id_type=MESH_ID)
    pl.semaphore_wait(barrier, 8)
    slabs = [
        [
            remote(diag.at[b], dv.at[b, :, columns], ds.at[b, d], dr.at[b, d], around[d])
            for d in (0, 2, 1)
        ]
        for b in range(4)
    ]
    for b in (0, 2, 1, 3):
        for c in slabs[b]:
            c.start()

    def arrived(b):
        own[b].wait()
        for c in slabs[b]:
            c.wait_recv()

    def node(n, power):
        other = 1 + lax.rem(n + 1, 2)
        bit = lax.rem(lax.div(seg, power), 2) * (n >= 3).astype(jnp.int32)
        a, b = bit * other, (1 - bit) * other
        par = lax.rem(n + 1, 2)

        def rows(base, i, size):
            return pl.ds(pl.multiple_of(base + i * size, size), size)

        def crossing(to, there):
            s, d = bit * 1024, (1 - bit) * 1024
            if there:
                s, d = d, s
            half = 512 * bit
            if there:
                half = 512 - half
            src, dst = (0, other) if there else (other, other)
            list_ = [
                (st.at[src, rows(s, core, 128)], st.at[dst, rows(s, core, 128)]),
                (st.at[src, rows(s + 256, core, 128), 256:512], st.at[dst, rows(s + 256, core, 128), 256:512]),
                (st.at[src, rows(512, me, 64)], st.at[dst, rows(512, me, 64)]),
                (rh.at[src, rows(half, core, 256)], rh.at[dst, rows(half, core, 256)]),
                (st.at[src, rows(d, me, 64)], st.at[dst, rows(d, me, 64)]),
                (rh.at[src, rows(512 - half, core, 256)], rh.at[dst, rows(512 - half, core, 256)]),
            ]
            return [remote(u, v, xsend.at[par, i], xrecv.at[par, i], to) for i, (u, v) in enumerate(list_)]

        def whole(there):
            s, d, half = bit * 1024, (1 - bit) * 1024, 512 * bit
            if there:
                s, d, half = d, s, 512 - half
            src = 0 if there else other
            list_ = [
                (st.at[src, rows(s, 0, 512)], st.at[other, rows(s, 0, 512)]),
                (st.at[src, rows(512, 0, 512)], st.at[other, rows(512, 0, 512)]),
                (rh.at[src, rows(half, 0, 512)], rh.at[other, rows(half, 0, 512)]),
                (st.at[src, rows(d, 0, 512)], st.at[other, rows(d, 0, 512)]),
                (rh.at[src, rows(512 - half, 0, 512)], rh.at[other, rows(512 - half, 0, 512)]),
            ]
            return [remote(u, v, xsend.at[par, i], xrecv.at[par, i], sibling) for i, (u, v) in enumerate(list_)]

        came = crossing(sibling, False)

        s_, d_, half_ = bit * 1024, (1 - bit) * 1024, 512 * bit
        got = [
            st.at[other, rows(s_, core, 128)],
            st.at[other, rows(s_ + 256, core, 128), 256:512],
            st.at[other, rows(512, me, 64)],
            rh.at[other, rows(half_, core, 256)],
            st.at[other, rows(d_, me, 64)],
            rh.at[other, rows(512 - half_, core, 256)],
        ]

        def to_sibling(i, ref):
            return remote(ref, ref, csend.at[par, i], crecv.at[par, i], sibling)

        def round_z(kind):
            i = 2 + 2 * kind
            return [
                remote(got[i], got[i], zsend.at[par, kind, d], zrecv.at[par, kind, d], around[d])
                for d in range(3)
            ]

        def from_z(kind):
            base = 512 if kind == 0 else d_
            out = []
            for d in range(3):
                owner = lax.rem(col + 3 - d, 4) * 2 + core
                ref = st.at[other, rows(base, owner, 64)]
                out.append(to_sibling(6 + 3 * kind + d, ref))
            return out

        direct = [to_sibling(i, got[i]) for i in range(6)]
        far = n >= 4

        def hook(j):
            @pl.when(far & (j == 1))
            def _():
                came[2].wait_recv()
                for c in round_z(0):
                    c.start()
                direct[2].start()

            @pl.when(far & (j == 2))
            def _():
                came[3].wait_recv()
                direct[3].start()

            @pl.when(far & (j == 3))
            def _():
                came[4].wait_recv()
                for c in round_z(1):
                    c.start()
                direct[4].start()
                for c, onward in zip(round_z(0), from_z(0)):
                    c.wait_recv()
                    onward.start()

        @pl.when(n == 0)
        def _():
            arrived(0)
            p[...] = dv[0]

        @pl.when(n == 1)
        def _():
            arrived(2)
            p[...] = dv[2]

        @pl.when(n == 2)
        def _():
            arrived(1)
            arrived(3)

        @pl.when(n == 3)
        def _():
            for c in whole(True):
                c.start()
            whole(False)[0].wait_recv()

        for level in range(1, 5):

            @pl.when(n == 3 + level)
            def _(level=level):
                pl.semaphore_wait(ready.at[level], 5)
                for c in crossing(across[level - 1], True):
                    c.start()

        @pl.when(far & (n < 8))
        def _():
            for i in (0, 1):
                came[i].wait_recv()
                direct[i].start()
            for i in (0, 1):
                direct[i].wait_recv()

        @pl.when((n >= 2) & (n < 8))
        def _():
            p[...] = st[a, 1024:1536, :] + st[b, 0:512, :]

        @pl.when(n == 2)
        def _():
            p[...] = p[...] + dv[1]

        @pl.when(n == 8)
        def _():
            p[...] = st[0, 1024:1536, :]

        p[256:512, 0:256] = p[0:256, 256:512].T
        invert(p, lambda j: pl.when(n < 8)(lambda: hook(j)))

        @pl.when(n < 8)
        def _():
            @pl.when(n == 0)
            def _():
                loads[0].wait()
                loads[1].wait()
                loads[4].wait()

            @pl.when(n == 1)
            def _():
                loads[2].wait()
                loads[3].wait()

            @pl.when(n < 2)
            def _():
                q = 2 * n
                has_left = 1.0 - ((n == 0) & (seg == 0)).astype(F32)
                et[512:1024, :] = lv[q + 1]
                e[:, 0:512] = lv[q] * has_left
                et[0:512, :] = e[:, 0:512].T
                e[:, 512:1024] = et[512:1024, :].T
                f[...] = rv[q]
                st[q] = jnp.zeros((1536, 512), F32)
                rh[q] = jnp.zeros((1024, 128), F32)

            @pl.when(n == 3)
            def _():
                for c in whole(False)[1:3]:
                    c.wait_recv()

            @pl.when(far)
            def _():
                for c in direct[2:4] + from_z(0):
                    c.wait_recv()

            @pl.when(n >= 2)
            def _():
                et[0:512, :] = st[a, 512:1024, :]
                e[:, 512:1024] = st[b, 512:1024, :]
                e[:, 0:512] = et[0:512, :].T
                et[512:1024, :] = e[:, 512:1024].T
                f[...] = rh[a, 512:1024, :] + rh[b, 0:512, :]

            @pl.when(n == 2)
            def _():
                f[...] = f[...] + rv[1]

            for q, part in enumerate(pieces(p[...])):
                p3[q] = part

            def tile(i, c):
                k = at(i, 256)
                out = dot(beside(p3[0], p3[1], p3[2]), below(*pieces(e[:, k])))
                gg[n, 0, :, k], gg[n, 1, :, k], gl[:, k] = pieces(out)
                return c

            lax.fori_loop(0, 4, tile, 0)
            fh, fm, _ = pieces(f[...])
            out = dot(
                jnp.concatenate([p3[0], p3[1], p3[0]], axis=1), jnp.concatenate([fh, fh, fm], axis=0)
            )
            gf[n] = out
            fp[0], fp[1], _ = pieces(out)

            @pl.when(n == 3)
            def _():
                for c in whole(False)[3:]:
                    c.wait_recv()
                for c in whole(True):
                    c.wait_send()

            @pl.when(far)
            def _():
                came[5].wait_recv()
                direct[5].start()
                for c, onward in zip(round_z(1), from_z(1)):
                    c.wait_recv()
                    onward.start()
                for c in direct[4:6] + from_z(1):
                    c.wait_recv()
                for c in crossing(sibling, True) + direct + round_z(0) + round_z(1) + from_z(0) + from_z(1):
                    c.wait_send()

            @pl.when(n >= 2)
            def _():
                r = pl.ds(pl.multiple_of((1 - bit) * 1024, 512), 512)
                st[0, r, :] = st[other, r, :]
                r = pl.ds(pl.multiple_of((1 - bit) * 512, 512), 512)
                rh[0, r, :] = rh[other, r, :]

            @pl.when(n == 2)
            def _():
                st[0, 1024:1536, :] = st[0, 1024:1536, :] + dv[3]
                rh[0, 512:1024, :] = rh[0, 512:1024, :] + rv[3]

            t = 2 * (n == 1).astype(jnp.int32)

            def term(i, k):
                k = at(k, 256)
                return dot(beside(*pieces(et[at(i, 256), :])), below(gg[n, 0, :, k], gg[n, 1, :, k], gl[:, k]))

            def corner(q, c):
                i, k = q // 2, at((q + 1) // 2, 256)
                st[t, at(i + 4, 256), k] = st[t, at(i + 4, 256), k] - term(i + 2, (q + 1) // 2 + 2)
                return c

            lax.fori_loop(0, 3, corner, 0)
            st[t, 1280:1536, 0:256] = st[t, 1024:1280, 256:512].T

            @pl.when(n < 7)
            def _():
                def corner(q, c):
                    i, k = q // 2, at((q + 1) // 2, 256)
                    st[t, at(i, 256), k] = st[t, at(i, 256), k] - term(i, (q + 1) // 2)
                    return c

                lax.fori_loop(0, 3, corner, 0)
                st[t, 256:512, 0:256] = st[t, 0:256, 256:512].T

                def square(q, c):
                    i, k = q // 2, q % 2
                    st[t, at(i + 2, 256), at(k, 256)] = -term(i, k + 2)
                    return c

                lax.fori_loop(0, 4, square, 0)

            def side(i, c):
                r = at(i, 256)
                h, m, _ = pieces(et[r, :])
                rh[t, r, :] = rh[t, r, :] - dot(
                    jnp.concatenate([h, m, h], axis=1), jnp.concatenate([fp[0], fp[0], fp[1]], axis=0)
                )
                return c

            lax.fori_loop(0, 4, side, 0)
            for level in range(1, 5):

                @pl.when(n == level + 1)
                def _(level=level):
                    for peer in [sibling, across[level - 1]] + around:
                        pl.semaphore_signal(
                            ready.at[level], inc=1, device_id=peer, device_id_type=MESH_ID
                        )

        return power * (1 + (n >= 3).astype(jnp.int32))

    lax.fori_loop(0, 9, node, jnp.int32(1))
    for b in range(4):
        for c in slabs[b]:
            c.wait_send()
    xs[0:512, :] = jnp.zeros((512, 128), F32)
    last = dot(beside(*pieces(p[...])), below(*pieces(rh[0, 512:1024, :])))
    xs[512:1024, :] = last
    x[3] = jnp.zeros((512, 128), F32)

    def back(i, power):
        n = 7 - i
        h, m, _ = pieces(xs[...])
        middle = gf[n] - dot(
            jnp.concatenate([gg[n, 0], gg[n, 1], gg[n, 0]], axis=1), jnp.concatenate([h, h, m], axis=0)
        )

        @pl.when(n >= 3)
        def _():
            bit = lax.rem(lax.div(seg, power), 2)
            xs[pl.ds(pl.multiple_of((1 - bit) * 512, 512), 512), :] = middle

        @pl.when(n == 2)
        def _():
            x[3] = xs[512:1024, :]
            x[1] = middle
            keep[...] = xs[0:512, :]
            xs[0:512, :] = middle

        @pl.when(n == 1)
        def _():
            x[2] = middle
            xs[512:1024, :] = xs[0:512, :]
            xs[0:512, :] = keep[...]

        @pl.when(n == 0)
        def _():
            x[0] = middle

        return power // (1 + (n > 3).astype(jnp.int32))

    lax.fori_loop(0, 8, back, jnp.int32(16))


def on_device(diagonal, lower, right_side):
    dma = pltpu.SemaphoreType.DMA
    vmem = pltpu.VMEM
    return pl.pallas_call(
        kernel,
        out_shape=jax.ShapeDtypeStruct((4, 512, 128), F32),
        in_specs=[pl.BlockSpec(memory_space=pl.ANY)] * 3,
        out_specs=pl.BlockSpec(memory_space=pltpu.VMEM),
        scratch_shapes=[
            vmem((4, 512, 512), F32), vmem((4, 512, 512), F32), vmem((4, 512, 128), F32),
            vmem((3, 1536, 512), F32), vmem((3, 1024, 128), F32),
            vmem((512, 512), F32), vmem((3, 512, 512), BF), vmem((512, 1024), F32),
            vmem((512, 128), F32), vmem((1024, 512), F32),
            vmem((8, 2, 512, 1024), BF), vmem((512, 1024), BF), vmem((8, 512, 128), F32),
            vmem((2, 512, 128), BF), vmem((1024, 128), F32), vmem((512, 128), F32),
            dma((9,)), dma((4, 3)), dma((4, 3)),
            dma((2, 6)), dma((2, 6)), dma((2, 2, 3)), dma((2, 2, 3)), dma((2, 12)), dma((2, 12)),
            pltpu.SemaphoreType.REGULAR((5,)),
        ],
        compiler_params=pltpu.CompilerParams(
            collective_id=0, has_side_effects=True, vmem_limit_bytes=64000 * 1024
        ),
    )(diagonal, lower, right_side)


def solution(mesh):
    in_specs = (P("seg", None, "col"), P("seg", None, None), P("seg", None, "col"))
    return jax.shard_map(
        on_device, mesh=mesh, in_specs=in_specs, out_specs=P("seg", None, "col"), check_vma=False
    )
```

time: 1970 us -> 329 us (0.17)
  other arithmetic: 1140 us -> 0 us
  matrix products: 331 us -> 0 us
  Pallas kernels: 0 us -> 326 us
  waiting for transfers between devices: 226 us -> 0 us
  local copies, waits for them, and re-layouts: 169 us -> 2.26 us
  starting transfers between devices: 49.7 us -> 0 us
  between operations: 32.2 us -> 0.01 us
    another operation x156 -> x0, other arithmetic: 1100 us -> none  [the longest x131 727 us: invert_spd(): factor = jnp.linalg.cholesky(matrix)]
    pallas_call x0 -> x1, Pallas kernels: none -> 326 us  [on_device(): pl.pallas_call(kernel, out_shape=jax.ShapeDtypeStruct((4, 512, 128), F32)...]
    dot_general x77 -> x0, matrix products: 210 us -> none  [matmul(): jnp.dot(left_hand, right_hand, precision=lax.Precision.HIGHEST, preferred...]
    all_gather x19 -> x0, waiting for transfers between devices: 165 us -> none  [the longest x5 95.3 us: on_device(): lax.all_gather(pivot_block, 'col', axis=1, tiled=True)]
    another operation x117 -> x0, matrix products: 121 us -> none  [the longest x63 66 us: invert_spd(): lax.linalg.triangular_solve(factor, identity, left_side=True, lower=True)]
    another operation x160 -> x0, local copies, waits for them, and re-layouts: 118 us -> none  [the longest x118 105 us: invert_spd(): lax.linalg.triangular_solve(factor, identity, left_side=True, lower=True)]
    ppermute x12 -> x0, waiting for transfers between devices: 59.6 us -> none  [passed_along(): return lax.ppermute(shard, axis, pairs)]
    ppermute x12 -> x0, starting transfers between devices: 47.3 us -> none  [passed_along(): return lax.ppermute(shard, axis, pairs)]
  transfers between devices with their start and end apart: 31 -> 0, of which waited for: 16 -> 0; matrix products, arithmetic and copies ran while one was open for 46% -> 0% of each run, Pallas kernels for 0% -> 0%
where the time goes in v3:
time: 329 us; the launch traced here: 328 us
  Pallas kernels  326 us (99%)
    pallas_call x1, Pallas kernels, on_device(): pl.pallas_call(kernel, out_shape=jax.ShapeDtypeStruct((4, 512, 128), F32)...  326 us

profile of v3, /device:TPU:1, one launch (start us, length us, event | category | flops | bytes accessed | tf_op | source)
XLA Modules:
  0.0 328.4 jit_solution(8227099950256314285)
XLA Ops:
  0.0 326.2 %shard_map.37 = f32[4,512,128]{2,1,0:T(8,128)} custom-call(f32[4,512,128]{2,1,0:T(8,128)} %diag.1, f32[4,512,512]{2,1,0:T(8,128)} %low.1, f32[4,512,128]{2,1,0:T(8,128)} %right.1), custom_call_target="tpu_custom_call" | custom-call | tf_op jit(solution)/shard_map/pallas_call | solution.py:515
  326.2 2.3 copy.5

commit v4 on v3

--- a/solution.py
+++ b/solution.py
@@ -154,10 +154,17 @@
     for peer in [sibling] + around + across:
         pl.semaphore_signal(barrier, inc=1, device_id=peer, device_id_type=MESH_ID)
     pl.semaphore_wait(barrier, 8)
+    upper = lax.div(col, 2)
+    third = (1 - upper) * (3 - col) + upper * (col - 2)
+    shares = [
+        pl.ds(pl.multiple_of(upper * 256, 256), 256),
+        pl.ds(pl.multiple_of(third * 128, 128), 128),
+    ]
     slabs = [
         [
-            remote(diag.at[b], dv.at[b, :, columns], ds.at[b, d], dr.at[b, d], around[d])
+            remote(diag.at[b, r], dv.at[b, r, columns], ds.at[b, d, i], dr.at[b, d, i], around[d])
             for d in (0, 2, 1)
+            for i, r in enumerate(shares)
         ]
         for b in range(4)
     ]
@@ -169,6 +176,8 @@
         own[b].wait()
         for c in slabs[b]:
             c.wait_recv()
+        dv[b, 0:128, 384:512] = dv[b, 384:512, 0:128].T
+        dv[b, 128:256, 256:384] = dv[b, 256:384, 128:256].T
 
     def node(n, power):
         other = 1 + lax.rem(n + 1, 2)
@@ -179,7 +188,7 @@
         def rows(base, i, size):
             return pl.ds(pl.multiple_of(base + i * size, size), size)
 
-        def crossing(to, there):
+        def crossing(to, there, bit=bit, other=other, par=par):
             s, d = bit * 1024, (1 - bit) * 1024
             if there:
                 s, d = d, s
@@ -197,7 +206,7 @@
             ]
             return [remote(u, v, xsend.at[par, i], xrecv.at[par, i], to) for i, (u, v) in enumerate(list_)]
 
-        def whole(there):
+        def whole(there, bit=bit, other=other, par=par):
             s, d, half = bit * 1024, (1 - bit) * 1024, 512 * bit
             if there:
                 s, d, half = d, s, 512 - half
@@ -270,6 +279,29 @@
 
         @pl.when(n == 0)
         def _():
+            loads[0].wait()
+            loads[1].wait()
+            loads[4].wait()
+
+        @pl.when(n == 1)
+        def _():
+            loads[2].wait()
+            loads[3].wait()
+
+        @pl.when(n < 2)
+        def _():
+            q = 2 * n
+            has_left = 1.0 - ((n == 0) & (seg == 0)).astype(F32)
+            et[512:1024, :] = lv[q + 1]
+            e[:, 0:512] = lv[q] * has_left
+            et[0:512, :] = e[:, 0:512].T
+            e[:, 512:1024] = et[512:1024, :].T
+            f[...] = rv[q]
+            st[q] = jnp.zeros((1536, 512), F32)
+            rh[q] = jnp.zeros((1024, 128), F32)
+
+        @pl.when(n == 0)
+        def _():
             arrived(0)
             p[...] = dv[0]
 
@@ -285,17 +317,7 @@
 
         @pl.when(n == 3)
         def _():
-            for c in whole(True):
-                c.start()
             whole(False)[0].wait_recv()
-
-        for level in range(1, 5):
-
-            @pl.when(n == 3 + level)
-            def _(level=level):
-                pl.semaphore_wait(ready.at[level], 5)
-                for c in crossing(across[level - 1], True):
-                    c.start()
 
         @pl.when(far & (n < 8))
         def _():
@@ -322,29 +344,6 @@
 
         @pl.when(n < 8)
         def _():
-            @pl.when(n == 0)
-            def _():
-                loads[0].wait()
-                loads[1].wait()
-                loads[4].wait()
-
-            @pl.when(n == 1)
-            def _():
-                loads[2].wait()
-                loads[3].wait()
-
-            @pl.when(n < 2)
-            def _():
-                q = 2 * n
-                has_left = 1.0 - ((n == 0) & (seg == 0)).astype(F32)
-                et[512:1024, :] = lv[q + 1]
-                e[:, 0:512] = lv[q] * has_left
-                et[0:512, :] = e[:, 0:512].T
-                e[:, 512:1024] = et[512:1024, :].T
-                f[...] = rv[q]
-                st[q] = jnp.zeros((1536, 512), F32)
-                rh[q] = jnp.zeros((1024, 128), F32)
-
             @pl.when(n == 3)
             def _():
                 for c in whole(False)[1:3]:
@@ -421,24 +420,46 @@
                 k = at(k, 256)
                 return dot(beside(*pieces(et[at(i, 256), :])), below(gg[n, 0, :, k], gg[n, 1, :, k], gl[:, k]))
 
-            def corner(q, c):
-                i, k = q // 2, at((q + 1) // 2, 256)
-                st[t, at(i + 4, 256), k] = st[t, at(i + 4, 256), k] - term(i + 2, (q + 1) // 2 + 2)
+            following = power * (1 + (n >= 3).astype(jnp.int32))
+            sends = (n >= 2) & (n < 7)
+            turn = lax.rem(lax.div(seg, following), 2)
+            first = 1 - turn * sends.astype(jnp.int32)
+            to = dict(bit=turn, other=1 + lax.rem(n, 2), par=lax.rem(n, 2))
+
+            def send(part):
+                @pl.when(n == 2)
+                def _():
+                    for c in whole(True, **to)[:1] if part == 0 else whole(True, **to)[1:]:
+                        c.start()
+
+                for level in range(1, 5):
+
+                    @pl.when(n == 2 + level)
+                    def _(level=level):
+                        out = crossing(across[level - 1], True, **to)
+                        if part == 0:
+                            pl.semaphore_wait(ready.at[level], 5)
+                        for c in out[:2] if part == 0 else out[2:]:
+                            c.start()
+
+            def corners(turned, c):
+                w = first + turned * (1 - 2 * first)
+
+                def corner(q, c):
+                    i, k = q // 2 + 4 * w, (q + 1) // 2
+                    r = at(i, 256)
+                    st[t, r, at(k, 256)] = st[t, r, at(k, 256)] - term(q // 2 + 2 * w, k + 2 * w)
+                    return c
+
+                lax.fori_loop(0, 3, corner, 0)
+                st[t, at(4 * w + 1, 256), 0:256] = st[t, at(4 * w, 256), 256:512].T
+                pl.when(turned == 0)(lambda: send(0))
                 return c
 
-            lax.fori_loop(0, 3, corner, 0)
-            st[t, 1280:1536, 0:256] = st[t, 1024:1280, 256:512].T
+            lax.fori_loop(0, 2 - (n == 7).astype(jnp.int32), corners, 0)
 
             @pl.when(n < 7)
             def _():
-                def corner(q, c):
-                    i, k = q // 2, at((q + 1) // 2, 256)
-                    st[t, at(i, 256), k] = st[t, at(i, 256), k] - term(i, (q + 1) // 2)
-                    return c
-
-                lax.fori_loop(0, 3, corner, 0)
-                st[t, 256:512, 0:256] = st[t, 0:256, 256:512].T
-
                 def square(q, c):
                     i, k = q // 2, q % 2
                     st[t, at(i + 2, 256), at(k, 256)] = -term(i, k + 2)
@@ -455,6 +476,7 @@
                 return c
 
             lax.fori_loop(0, 4, side, 0)
+            send(1)
             for level in range(1, 5):
 
                 @pl.when(n == level + 1)
@@ -524,7 +546,7 @@
             vmem((512, 128), F32), vmem((1024, 512), F32),
             vmem((8, 2, 512, 1024), BF), vmem((512, 1024), BF), vmem((8, 512, 128), F32),
             vmem((2, 512, 128), BF), vmem((1024, 128), F32), vmem((512, 128), F32),
-            dma((9,)), dma((4, 3)), dma((4, 3)),
+            dma((9,)), dma((4, 3, 2)), dma((4, 3, 2)),
             dma((2, 6)), dma((2, 6)), dma((2, 2, 3)), dma((2, 2, 3)), dma((2, 12)), dma((2, 12)),
             pltpu.SemaphoreType.REGULAR((5,)),
         ],

time: 329 us -> 300 us (0.912)
  Pallas kernels: 326 us -> 297 us
    pallas_call x1, Pallas kernels: 326 us -> 297 us  [on_device(): pl.pallas_call(kernel, out_shape=jax.ShapeDtypeStruct((4, 512, 128), F32)...]
where the time goes in v4:
time: 300 us
  Pallas kernels  297 us (99%)
    pallas_call x1, Pallas kernels, on_device(): pl.pallas_call(kernel, out_shape=jax.ShapeDtypeStruct((4, 512, 128), F32)...  297 us

profile of v4, /device:TPU:1, one launch (start us, length us, event | category | flops | bytes accessed | tf_op | source)
XLA Modules:
  0.0 299.6 jit_solution(16942496215034259248)
XLA Ops:
  0.0 297.3 %shard_map.37 = f32[4,512,128]{2,1,0:T(8,128)} custom-call(f32[4,512,128]{2,1,0:T(8,128)} %diag.1, f32[4,512,512]{2,1,0:T(8,128)} %low.1, f32[4,512,128]{2,1,0:T(8,128)} %right.1), custom_call_target="tpu_custom_call" | custom-call | tf_op jit(solution)/shard_map/pallas_call | solution.py:537
  297.3 2.3 copy.5

commit v5 on v4

--- a/solution.py
+++ b/solution.py
@@ -108,23 +108,32 @@
     return (y * 4 + x) * 2 + core
 
 
-def invert(p, hook):
-    def step(j, c):
-        hook(j)
+def invert(p, hook, started, joined):
+    def step(j, late):
         s = at(j, 128)
         w = invert128(p[s, s])
+        if late:
+            started()
         rowid = lax.broadcasted_iota(jnp.int32, (512, 1), 0) // 128
         u6 = beside(*pieces(jnp.where(rowid == j, 0.0, p[:, s])))
         w6 = beside(*pieces(w))
         t = dot(w6, below(*pieces(p[s, :])))
         here = lax.broadcasted_iota(jnp.int32, (1, 512), 1) // 128 == j
         t = jnp.where(here, jnp.concatenate([w] * 4, axis=1), t)
+        if late:
+            joined()
         for n in (slice(0, 256), slice(256, 512)):
             p[:, n] = jnp.where(here[:, n], 0.0, p[:, n]) - dot(u6, below(*pieces(t[:, n])))
         p[s, :] = t
+
+    step(0, True)
+
+    def later(j, c):
+        hook(j)
+        step(j, False)
         return c
 
-    lax.fori_loop(0, 4, step, 0)
+    lax.fori_loop(1, 4, later, 0)
 
 
 def kernel(
@@ -200,8 +209,8 @@
                 (st.at[src, rows(s, core, 128)], st.at[dst, rows(s, core, 128)]),
                 (st.at[src, rows(s + 256, core, 128), 256:512], st.at[dst, rows(s + 256, core, 128), 256:512]),
                 (st.at[src, rows(512, me, 64)], st.at[dst, rows(512, me, 64)]),
+                (st.at[src, rows(d, me, 64)], st.at[dst, rows(d, me, 64)]),
                 (rh.at[src, rows(half, core, 256)], rh.at[dst, rows(half, core, 256)]),
-                (st.at[src, rows(d, me, 64)], st.at[dst, rows(d, me, 64)]),
                 (rh.at[src, rows(512 - half, core, 256)], rh.at[dst, rows(512 - half, core, 256)]),
             ]
             return [remote(u, v, xsend.at[par, i], xrecv.at[par, i], to) for i, (u, v) in enumerate(list_)]
@@ -227,8 +236,8 @@
             st.at[other, rows(s_, core, 128)],
             st.at[other, rows(s_ + 256, core, 128), 256:512],
             st.at[other, rows(512, me, 64)],
+            st.at[other, rows(d_, me, 64)],
             rh.at[other, rows(half_, core, 256)],
-            st.at[other, rows(d_, me, 64)],
             rh.at[other, rows(512 - half_, core, 256)],
         ]
 
@@ -236,7 +245,7 @@
             return remote(ref, ref, csend.at[par, i], crecv.at[par, i], sibling)
 
         def round_z(kind):
-            i = 2 + 2 * kind
+            i = 2 + kind
             return [
                 remote(got[i], got[i], zsend.at[par, kind, d], zrecv.at[par, kind, d], around[d])
                 for d in range(3)
@@ -255,27 +264,36 @@
         far = n >= 4
 
         def hook(j):
-            @pl.when(far & (j == 1))
-            def _():
-                came[2].wait_recv()
-                for c in round_z(0):
-                    c.start()
-                direct[2].start()
-
-            @pl.when(far & (j == 2))
-            def _():
-                came[3].wait_recv()
-                direct[3].start()
-
-            @pl.when(far & (j == 3))
-            def _():
-                came[4].wait_recv()
-                for c in round_z(1):
-                    c.start()
-                direct[4].start()
-                for c, onward in zip(round_z(0), from_z(0)):
-                    c.wait_recv()
-                    onward.start()
+            for kind in (0, 1):
+
+                @pl.when(far & (n < 8) & (j == 1 + kind))
+                def _(kind=kind):
+                    came[2 + kind].wait_recv()
+                    for c in round_z(kind):
+                        c.start()
+                    direct[2 + kind].start()
+
+        def started():
+            @pl.when(far & (n < 8))
+            def _():
+                came[1].wait_recv()
+                direct[1].start()
+
+        def joined():
+            @pl.when(far & (n < 8))
+            def _():
+                direct[1].wait_recv()
+                p[256:512, 256:512] = st[a, 1280:1536, 256:512] + st[b, 256:512, 256:512]
+
+        def left_couplings(source):
+            et[0:512, :] = source
+            e[:, 0:512] = source.T
+
+        def right_couplings(source):
+            e[:, 512:1024] = source
+            et[512:1024, :] = source.T
+
+        merging = (n >= 2) & (n < 8)
 
         @pl.when(n == 0)
         def _():
@@ -319,15 +337,22 @@
         def _():
             whole(False)[0].wait_recv()
 
+        @pl.when(merging & (bit == 0))
+        def _():
+            left_couplings(st[0, 512:1024, :])
+
+        @pl.when(merging & (bit == 1))
+        def _():
+            right_couplings(st[0, 512:1024, :])
+
         @pl.when(far & (n < 8))
         def _():
-            for i in (0, 1):
-                came[i].wait_recv()
-                direct[i].start()
-            for i in (0, 1):
-                direct[i].wait_recv()
-
-        @pl.when((n >= 2) & (n < 8))
+            came[0].wait_recv()
+            direct[0].start()
+            direct[0].wait_recv()
+            p[0:256, :] = st[a, 1024:1280, :] + st[b, 0:256, :]
+
+        @pl.when((n == 2) | (n == 3))
         def _():
             p[...] = st[a, 1024:1536, :] + st[b, 0:512, :]
 
@@ -340,42 +365,67 @@
             p[...] = st[0, 1024:1536, :]
 
         p[256:512, 0:256] = p[0:256, 256:512].T
-        invert(p, lambda j: pl.when(n < 8)(lambda: hook(j)))
+        invert(p, hook, started, joined)
 
         @pl.when(n < 8)
         def _():
-            @pl.when(n == 3)
-            def _():
-                for c in whole(False)[1:3]:
-                    c.wait_recv()
-
-            @pl.when(far)
-            def _():
-                for c in direct[2:4] + from_z(0):
-                    c.wait_recv()
-
-            @pl.when(n >= 2)
-            def _():
-                et[0:512, :] = st[a, 512:1024, :]
-                e[:, 512:1024] = st[b, 512:1024, :]
-                e[:, 0:512] = et[0:512, :].T
-                et[512:1024, :] = e[:, 512:1024].T
-                f[...] = rh[a, 512:1024, :] + rh[b, 0:512, :]
-
-            @pl.when(n == 2)
-            def _():
-                f[...] = f[...] + rv[1]
-
             for q, part in enumerate(pieces(p[...])):
                 p3[q] = part
 
+            @pl.when(far)
+            def _():
+                came[4].wait_recv()
+                direct[4].start()
+                for c, onward in zip(round_z(0), from_z(0)):
+                    c.wait_recv()
+                    onward.start()
+
             def tile(i, c):
-                k = at(i, 256)
+                k = at(lax.rem(i + 2 * bit, 4), 256)
                 out = dot(beside(p3[0], p3[1], p3[2]), below(*pieces(e[:, k])))
                 gg[n, 0, :, k], gg[n, 1, :, k], gl[:, k] = pieces(out)
                 return c
 
-            lax.fori_loop(0, 4, tile, 0)
+            def half_of(i, c):
+                @pl.when((i == 1) & (n == 3))
+                def _():
+                    for c in whole(False)[1:]:
+                        c.wait_recv()
+
+                @pl.when((i == 1) & far)
+                def _():
+                    for c in [direct[2], direct[4]] + from_z(0):
+                        c.wait_recv()
+                    came[5].wait_recv()
+                    direct[5].start()
+
+                @pl.when((i == 1) & merging & (bit == 0))
+                def _():
+                    right_couplings(st[other, 512:1024, :])
+
+                @pl.when((i == 1) & merging & (bit == 1))
+                def _():
+                    left_couplings(st[other, 512:1024, :])
+
+                lax.fori_loop(2 * i, 2 * i + 2, tile, 0)
+                return c
+
+            lax.fori_loop(0, 2, half_of, 0)
+
+            @pl.when(far)
+            def _():
+                for c, onward in zip(round_z(1), from_z(1)):
+                    c.wait_recv()
+                    onward.start()
+
+            @pl.when(n >= 2)
+            def _():
+                f[...] = rh[a, 512:1024, :] + rh[b, 0:512, :]
+
+            @pl.when(n == 2)
+            def _():
+                f[...] = f[...] + rv[1]
+
             fh, fm, _ = pieces(f[...])
             out = dot(
                 jnp.concatenate([p3[0], p3[1], p3[0]], axis=1), jnp.concatenate([fh, fh, fm], axis=0)
@@ -385,19 +435,12 @@
 
             @pl.when(n == 3)
             def _():
-                for c in whole(False)[3:]:
-                    c.wait_recv()
                 for c in whole(True):
                     c.wait_send()
 
             @pl.when(far)
             def _():
-                came[5].wait_recv()
-                direct[5].start()
-                for c, onward in zip(round_z(1), from_z(1)):
-                    c.wait_recv()
-                    onward.start()
-                for c in direct[4:6] + from_z(1):
+                for c in [direct[3], direct[5]] + from_z(1):
                     c.wait_recv()
                 for c in crossing(sibling, True) + direct + round_z(0) + round_z(1) + from_z(0) + from_z(1):
                     c.wait_send()

time: 300 us -> 287 us (0.957)
  Pallas kernels: 297 us -> 285 us
    pallas_call x1, Pallas kernels: 297 us -> 285 us  [on_device(): pl.pallas_call(kernel, out_shape=jax.ShapeDtypeStruct((4, 512, 128), F32)...]
where the time goes in v5:
time: 287 us
  Pallas kernels  285 us (99%)
    pallas_call x1, Pallas kernels, on_device(): pl.pallas_call(kernel, out_shape=jax.ShapeDtypeStruct((4, 512, 128), F32)...  285 us

profile of v5, /device:TPU:1, one launch (start us, length us, event | category | flops | bytes accessed | tf_op | source)
XLA Modules:
  0.0 287.1 jit_solution(13576005592945669425)
XLA Ops:
  0.0 284.9 %shard_map.37 = f32[4,512,128]{2,1,0:T(8,128)} custom-call(f32[4,512,128]{2,1,0:T(8,128)} %diag.1, f32[4,512,512]{2,1,0:T(8,128)} %low.1, f32[4,512,128]{2,1,0:T(8,128)} %right.1), custom_call_target="tpu_custom_call" | custom-call | tf_op jit(solution)/shard_map/pallas_call | solution.py:580
  284.9 2.3 copy.5

commit v6 on v5

--- a/solution.py
+++ b/solution.py
@@ -43,15 +43,17 @@
     for k in range(count):
         first = W * k
         rows = panels[k]
-        cols = [jnp.broadcast_to(rows[:, first + p : first + p + 1], (W, 128)) for p in range(W)]
+        near = [i for i in (k + 1,) if i < count]
+        cols, wide = [], {i: [] for i in near}
+        for p in range(W):
+            cols.append(jnp.broadcast_to(rows[:, first + p : first + p + 1], (W, 128)))
+        for i in near:
+            for p in range(W):
+                wide[i].append(jnp.broadcast_to(panels[i][:, first + p : first + p + 1], (W, 128)))
         inside = (lane >= first) & (lane < first + W)
-        after = k + 1 if k + 1 < count else None
-        if after is not None:
-            wide = [
-                jnp.broadcast_to(panels[after][:, first + p : first + p + 1], (W, 128)) for p in range(W)
-            ]
-        rest = [i for i in range(count) if i not in (k, after)]
-        left = beside(*pieces(jnp.concatenate([panels[i] for i in rest], axis=0)))
+        rest = [i for i in range(count) if i != k and i not in near]
+        if rest:
+            left = beside(*pieces(jnp.concatenate([panels[i] for i in rest], axis=0)))
         rows = jnp.where(inside, (lane - first == sub).astype(F32), rows)
         diag = cols[0][0:1, :]
         for p in range(W):
@@ -59,34 +61,32 @@
             here = sub == p
             column = cols[p]
             for j in range(p + 1, W):
+                scaled = cols[j][p : p + 1, :] * pivot
+                moved = cols[j] - column * scaled
                 if j == p + 1:
-                    moved = cols[j] - (column * cols[j][p : p + 1, :]) * pivot
                     diag = moved[j : j + 1, :]
-                    cols[j] = jnp.where(here, cols[j][p : p + 1, :] * pivot, moved)
-                else:
-                    scaled = cols[j][p : p + 1, :] * pivot
-                    cols[j] = jnp.where(here, scaled, cols[j] - column * scaled)
+                cols[j] = jnp.where(here, scaled, moved)
             scaled = rows[p : p + 1, :] * pivot
             rows = jnp.where(here, scaled, rows - column * scaled)
-        if after is not None:
-            acc = jnp.where(inside, 0.0, panels[after])
-            for p in range(W):
-                acc = acc - wide[p] * rows[p : p + 1, :]
-        padded = [
-            jnp.concatenate(
-                [jnp.zeros((first, 128), BF)] * (first > 0)
-                + [q]
-                + [jnp.zeros((112 - first, 128), BF)] * (first < 112),
-                axis=0,
-            )
-            for q in pieces(rows)
-        ]
-        delta = dot(left, below(*padded))
-        for n, i in enumerate(rest):
-            panels[i] = jnp.where(inside, 0.0, panels[i]) - delta[W * n : W * n + W]
+        if rest:
+            padded = [
+                jnp.concatenate(
+                    [jnp.zeros((first, 128), BF)] * (first > 0)
+                    + [q]
+                    + [jnp.zeros((112 - first, 128), BF)] * (first < 112),
+                    axis=0,
+                )
+                for q in pieces(rows)
+            ]
+            delta = dot(left, below(*padded))
+            for n, i in enumerate(rest):
+                panels[i] = jnp.where(inside, 0.0, panels[i]) - delta[W * n : W * n + W]
+        for i in near:
+            sums = [wide[i][p] * rows[p : p + 1, :] for p in range(4)]
+            for p in range(4, W):
+                sums[p % 4] = sums[p % 4] + wide[i][p] * rows[p : p + 1, :]
+            panels[i] = jnp.where(inside, 0.0, panels[i]) - ((sums[0] + sums[1]) + (sums[2] + sums[3]))
         panels[k] = rows
-        if after is not None:
-            panels[after] = acc
     return jnp.concatenate(panels, axis=0)
 
 
@@ -407,7 +407,8 @@
                 def _():
                     left_couplings(st[other, 512:1024, :])
 
-                lax.fori_loop(2 * i, 2 * i + 2, tile, 0)
+                tile(2 * i, 0)
+                tile(2 * i + 1, 0)
                 return c
 
             lax.fori_loop(0, 2, half_of, 0)
@@ -494,7 +495,8 @@
                     st[t, r, at(k, 256)] = st[t, r, at(k, 256)] - term(q // 2 + 2 * w, k + 2 * w)
                     return c
 
-                lax.fori_loop(0, 3, corner, 0)
+                for q in range(3):
+                    corner(q, 0)
                 st[t, at(4 * w + 1, 256), 0:256] = st[t, at(4 * w, 256), 256:512].T
                 pl.when(turned == 0)(lambda: send(0))
                 return c
@@ -508,7 +510,7 @@
                     st[t, at(i + 2, 256), at(k, 256)] = -term(i, k + 2)
                     return c
 
-                lax.fori_loop(0, 4, square, 0)
+                lax.fori_loop(0, 4, square, 0, unroll=4)
 
             def side(i, c):
                 r = at(i, 256)
@@ -518,7 +520,7 @@
                 )
                 return c
 
-            lax.fori_loop(0, 4, side, 0)
+            lax.fori_loop(0, 4, side, 0, unroll=4)
             send(1)
             for level in range(1, 5):
 

time: 287 us -> 277 us (0.965)
  Pallas kernels: 285 us -> 275 us
    pallas_call x1, Pallas kernels: 285 us -> 275 us  [on_device(): pl.pallas_call(kernel, out_shape=jax.ShapeDtypeStruct((4, 512, 128), F32)...]
where the time goes in v6:
time: 277 us
  Pallas kernels  275 us (99%)
    pallas_call x1, Pallas kernels, on_device(): pl.pallas_call(kernel, out_shape=jax.ShapeDtypeStruct((4, 512, 128), F32)...  275 us

profile of v6, /device:TPU:1, one launch (start us, length us, event | category | flops | bytes accessed | tf_op | source)
XLA Modules:
  0.0 276.9 jit_solution(12353587197726709767)
XLA Ops:
  0.0 274.7 %shard_map.37 = f32[4,512,128]{2,1,0:T(8,128)} custom-call(f32[4,512,128]{2,1,0:T(8,128)} %diag.1, f32[4,512,512]{2,1,0:T(8,128)} %low.1, f32[4,512,128]{2,1,0:T(8,128)} %right.1), custom_call_target="tpu_custom_call" | custom-call | tf_op jit(solution)/shard_map/pallas_call | solution.py:582
  274.7 2.3 copy.5
